TPU v7x, 128 devices: a whole 4x4x4 slice. The times are simulated.
128 devices in a mesh: lon: 16 (over x, z_hi, core), lat: 8 (over y, z_lo).
Axes of the slice: x: 4, y: 4, z: 4 (z_hi: 2, z_lo: 2; z = z_hi * 2 + z_lo), core: 2. Of those that a mesh axis runs over, the one named last changes fastest.
Arguments:
- fields: bfloat16 [4, 2, 1024, 4096], P(None, None, 'lat', 'lon'), may hold values from -6 to 6
- shifts: int32 [2, 64], P(None, 'lat'), may hold values from 0 to 4095
- fractions: float32 [2, 1024, 4096], P(None, 'lat', 'lon'), may hold values from 0 to 1
- helm_coef: float32 [2], replicated, may hold values from 1 to 16
Outputs:
- fields_out: bfloat16 [4, 2, 1024, 4096], P(None, None, 'lat', 'lon')
All inputs are finite; a program needn't handle non-finite values.
Results may differ from a plain program's by a relative error of at most 0.0044.
The roundings to bfloat16 on the way count: a program that leaves them out, or rounds other values in their place, can miss the bound.
Values may be sent and summed in bfloat16 or wider, within the bound.
A program may use at most 64 MiB of HBM per device.

v0:
```python
import jax
import jax.numpy as jnp
from jax import lax
from jax.sharding import PartitionSpec as P

STEPS = 2
SWEEPS = 8


TAU = 0.5


def with_halo(x, sides, width):
    for axis, dim in sides:
        size, length = (lax.axis_size(axis), x.shape[dim])
        up = [(i, (i + 1) % size) for i in range(size)]
        down = [(j, i) for i, j in up]
        last = lax.slice_in_dim(x, length - width, length, axis=dim)
        first = lax.slice_in_dim(x, 0, width, axis=dim)
        before = lax.ppermute(last, axis, up)
        after = lax.ppermute(first, axis, down)
        x = jnp.concatenate([before, x, after], axis=dim)
    return x


def shifted(value, axis, steps):
    count = lax.axis_size(axis)
    pairs = [(source, (source + steps) % count) for source in range(count)]
    return lax.ppermute(value, axis, pairs)


def cubic_weights(fraction):
    return (
        -fraction * (fraction - 1.0) * (fraction - 2.0) / 6.0,
        (fraction + 1.0) * (fraction - 1.0) * (fraction - 2.0) / 2.0,
        -(fraction + 1.0) * fraction * (fraction - 2.0) / 2.0,
        (fraction + 1.0) * fraction * (fraction - 1.0) / 6.0,
    )


def lat_keep(padded, rim_width, lat_dim):
    row_count = padded.shape[lat_dim]
    inner_rows = row_count - 2 * rim_width
    lat_total = inner_rows * lax.axis_size("lat")
    global_row = lax.axis_index("lat") * inner_rows + lax.iota(jnp.int32, row_count) - rim_width
    keep_mask = ((global_row >= 0) & (global_row < lat_total)).astype(padded.dtype)
    mask_shape = [1] * padded.ndim
    mask_shape[lat_dim] = row_count
    return padded * keep_mask.reshape(mask_shape)


def cell_rimmed(current):
    return with_halo(current, (("lon", 3),), 2)


def upstream_rows(current, shift_dev, frac_dev):
    cell_count = current.shape[3]
    row_count = current.shape[2]
    block_count = shift_dev.shape[0]
    block_rows = row_count // block_count
    tile_shift = shift_dev // cell_count
    cell_shift = shift_dev % cell_count
    tile_row = jnp.repeat(tile_shift, block_rows)
    rimmed = cell_rimmed(current)
    lon_count = lax.axis_size("lon")

    def cycle_step(turn_index, carry):
        moving, near_tile, far_tile = carry
        pick_near = (tile_row == turn_index)[None, None, :, None]
        pick_far = (tile_row + 1 == turn_index)[None, None, :, None]
        near_tile = jnp.where(pick_near, moving, near_tile)
        far_tile = jnp.where(pick_far, moving, far_tile)
        moving = shifted(moving, "lon", 1)
        return (moving, near_tile, far_tile)

    moving, near_tile, far_tile = lax.fori_loop(0, lon_count, cycle_step, (rimmed, rimmed, rimmed))
    far_tile = jnp.where((tile_row + 1 == lon_count)[None, None, :, None], moving, far_tile)
    window = jnp.concatenate([far_tile[..., :cell_count], near_tile], axis=3)
    window_parts = jnp.moveaxis(
        window.reshape(window.shape[0], window.shape[1], block_count, block_rows, window.shape[3]),
        2,
        0,
    )
    block_fracs = frac_dev.reshape(block_count, block_rows, cell_count)

    def interp_block(window_part, block_frac, block_offset):
        node_weights = cubic_weights(block_frac)
        accumulated = jnp.zeros(window_part.shape[:3] + (cell_count,), jnp.float32)
        for node_index in range(4):
            sampled = lax.dynamic_slice_in_dim(
                window_part, cell_count + 3 - node_index - block_offset, cell_count, axis=3
            )
            accumulated = accumulated + node_weights[node_index] * sampled.astype(jnp.float32)
        return accumulated.astype(jnp.bfloat16)

    advected = jax.vmap(interp_block)(window_parts, block_fracs, cell_shift)
    return jnp.moveaxis(advected, 0, 2).reshape(current.shape)


def four_neighbours(padded):
    return padded[:, 1:-1, 2:] + padded[:, 1:-1, :-2] + (padded[:, 2:, 1:-1] + padded[:, :-2, 1:-1])


def helmholtz(source, coefficient):
    diag_scale = 1.0 + 4.0 * coefficient
    potential = source
    for sweep_index in range(SWEEPS):
        padded = lat_keep(
            with_halo(potential.astype(jnp.bfloat16), (("lon", 2), ("lat", 1)), 1).astype(
                potential.dtype
            ),
            1,
            1,
        )
        potential = (source + coefficient * four_neighbours(padded)) / diag_scale
    return potential


def local(fields, shifts, fractions, helm_coef):
    coefficient = helm_coef[:, None, None]
    current = fields
    for step_index in range(STEPS):
        advected = upstream_rows(current, shifts[step_index], fractions[step_index])
        flux = advected.astype(jnp.float32)
        flux_pair = lat_keep(with_halo(advected[1:3], (("lon", 3), ("lat", 2)), 1), 1, 2).astype(
            jnp.float32
        )
        east_div = 0.5 * (flux_pair[0, :, 1:-1, 2:] - flux_pair[0, :, 1:-1, :-2])
        north_div = 0.5 * (flux_pair[1, :, 2:, 1:-1] - flux_pair[1, :, :-2, 1:-1])
        source = flux[0] - TAU * (east_div + north_div)
        potential = helmholtz(source, coefficient)
        phi_rimmed = lat_keep(
            with_halo(potential.astype(jnp.bfloat16), (("lon", 2), ("lat", 1)), 1).astype(
                potential.dtype
            ),
            1,
            1,
        )
        east_wind = flux[1] - TAU * (0.5 * (phi_rimmed[:, 1:-1, 2:] - phi_rimmed[:, 1:-1, :-2]))
        north_wind = flux[2] - TAU * (0.5 * (phi_rimmed[:, 2:, 1:-1] - phi_rimmed[:, :-2, 1:-1]))
        current = jnp.stack([potential, east_wind, north_wind, flux[3]]).astype(jnp.bfloat16)
    return current


def solution(mesh):
    return jax.shard_map(
        local,
        mesh=mesh,
        in_specs=(P(None, None, "lat", "lon"), P(None, "lat"), P(None, "lat", "lon"), P()),
        out_specs=P(None, None, "lat", "lon"),
        check_vma=False,
    )
```

profile of v0, /device:TPU:1, one launch (start us, length us, event | category | flops | bytes accessed | tf_op | source)
XLA Modules:
  0.0 861.7 jit_solution(10911203173169644819)
XLA Ops:
  11.7 192.2 %while.36 = (s32[]{:T(128)}, bf16[4,2,128,260]{2,0,3,1:T(4,128)(2,1)S(1)}, bf16[4,2,128,260]{2,0,3,1:T(4,128)(2,1)S(1)}, bf16[4,2,128,260]{2,0,3,1:T(4,128)(2,1)S(1)}, s32[8]{0:T(128)S(1)}, /*index=5*/s32[]{:T(128)}) while((s32[]{:T(128)}, bf16[4,2,128,260]{2,0,3,1:T(4,128)(2,1)S(1)}, bf16[4,2,128,260]{2,0,3,1:T(4,128)(2,1)S(1)}, ...), condition=%wide.region_1.2_spmd.clone, body=%wide.region_0.1_spmd.clone.sunk | while | flops 532866 | bytes 5859993 | solution.py:76
  47.3 5.9 collective-permute-done
  57.8 8.0 collective-permute-done
  68.2 10.1 %collective-permute-done = bf16[4,2,128,260]{2,0,3,1:T(4,128)(2,1)S(1)} collective-permute-done((bf16[4,2,128,260]{2,0,3,1:T(4,128)(2,1)S(1)}, bf16[4,2,128,260]{2,0,3,1:T(4,128)(2,1)S(1)}, u32[]{:S(2)}, u32[]{:S(2)}) %collective-permute-start) | collective-permute-done | bytes 532512 | tf_op jit(solution)/shard_map/while/body/eval_jaxpr/ppermute | solution.py:29
  79.3 11.5 %collective-permute-done = bf16[4,2,128,260]{2,0,3,1:T(4,128)(2,1)S(1)} collective-permute-done((bf16[4,2,128,260]{2,0,3,1:T(4,128)(2,1)S(1)}, bf16[4,2,128,260]{2,0,3,1:T(4,128)(2,1)S(1)}, u32[]{:S(2)}, u32[]{:S(2)}) %collective-permute-start) | collective-permute-done | bytes 532512 | tf_op jit(solution)/shard_map/while/body/eval_jaxpr/ppermute | solution.py:29
  91.9 11.5 %collective-permute-done = bf16[4,2,128,260]{2,0,3,1:T(4,128)(2,1)S(1)} collective-permute-done((bf16[4,2,128,260]{2,0,3,1:T(4,128)(2,1)S(1)}, bf16[4,2,128,260]{2,0,3,1:T(4,128)(2,1)S(1)}, u32[]{:S(2)}, u32[]{:S(2)}) %collective-permute-start) | collective-permute-done | bytes 532512 | tf_op jit(solution)/shard_map/while/body/eval_jaxpr/ppermute | solution.py:29
  104.4 11.5 %collective-permute-done = bf16[4,2,128,260]{2,0,3,1:T(4,128)(2,1)S(1)} collective-permute-done((bf16[4,2,128,260]{2,0,3,1:T(4,128)(2,1)S(1)}, bf16[4,2,128,260]{2,0,3,1:T(4,128)(2,1)S(1)}, u32[]{:S(2)}, u32[]{:S(2)}) %collective-permute-start) | collective-permute-done | bytes 532512 | tf_op jit(solution)/shard_map/while/body/eval_jaxpr/ppermute | solution.py:29
  117.0 11.5 %collective-permute-done = bf16[4,2,128,260]{2,0,3,1:T(4,128)(2,1)S(1)} collective-permute-done((bf16[4,2,128,260]{2,0,3,1:T(4,128)(2,1)S(1)}, bf16[4,2,128,260]{2,0,3,1:T(4,128)(2,1)S(1)}, u32[]{:S(2)}, u32[]{:S(2)}) %collective-permute-start) | collective-permute-done | bytes 532512 | tf_op jit(solution)/shard_map/while/body/eval_jaxpr/ppermute | solution.py:29
  129.6 11.5 %collective-permute-done = bf16[4,2,128,260]{2,0,3,1:T(4,128)(2,1)S(1)} collective-permute-done((bf16[4,2,128,260]{2,0,3,1:T(4,128)(2,1)S(1)}, bf16[4,2,128,260]{2,0,3,1:T(4,128)(2,1)S(1)}, u32[]{:S(2)}, u32[]{:S(2)}) %collective-permute-start) | collective-permute-done | bytes 532512 | tf_op jit(solution)/shard_map/while/body/eval_jaxpr/ppermute | solution.py:29
  142.1 11.5 %collective-permute-done = bf16[4,2,128,260]{2,0,3,1:T(4,128)(2,1)S(1)} collective-permute-done((bf16[4,2,128,260]{2,0,3,1:T(4,128)(2,1)S(1)}, bf16[4,2,128,260]{2,0,3,1:T(4,128)(2,1)S(1)}, u32[]{:S(2)}, u32[]{:S(2)}) %collective-permute-start) | collective-permute-done | bytes 532512 | tf_op jit(solution)/shard_map/while/body/eval_jaxpr/ppermute | solution.py:29
  154.7 11.5 %collective-permute-done = bf16[4,2,128,260]{2,0,3,1:T(4,128)(2,1)S(1)} collective-permute-done((bf16[4,2,128,260]{2,0,3,1:T(4,128)(2,1)S(1)}, bf16[4,2,128,260]{2,0,3,1:T(4,128)(2,1)S(1)}, u32[]{:S(2)}, u32[]{:S(2)}) %collective-permute-start) | collective-permute-done | bytes 532512 | tf_op jit(solution)/shard_map/while/body/eval_jaxpr/ppermute | solution.py:29
  167.3 11.5 %collective-permute-done = bf16[4,2,128,260]{2,0,3,1:T(4,128)(2,1)S(1)} collective-permute-done((bf16[4,2,128,260]{2,0,3,1:T(4,128)(2,1)S(1)}, bf16[4,2,128,260]{2,0,3,1:T(4,128)(2,1)S(1)}, u32[]{:S(2)}, u32[]{:S(2)}) %collective-permute-start) | collective-permute-done | bytes 532512 | tf_op jit(solution)/shard_map/while/body/eval_jaxpr/ppermute | solution.py:29
  179.8 11.5 %collective-permute-done = bf16[4,2,128,260]{2,0,3,1:T(4,128)(2,1)S(1)} collective-permute-done((bf16[4,2,128,260]{2,0,3,1:T(4,128)(2,1)S(1)}, bf16[4,2,128,260]{2,0,3,1:T(4,128)(2,1)S(1)}, u32[]{:S(2)}, u32[]{:S(2)}) %collective-permute-start) | collective-permute-done | bytes 532512 | tf_op jit(solution)/shard_map/while/body/eval_jaxpr/ppermute | solution.py:29
  192.4 11.5 %collective-permute-done = bf16[4,2,128,260]{2,0,3,1:T(4,128)(2,1)S(1)} collective-permute-done((bf16[4,2,128,260]{2,0,3,1:T(4,128)(2,1)S(1)}, bf16[4,2,128,260]{2,0,3,1:T(4,128)(2,1)S(1)}, u32[]{:S(2)}, u32[]{:S(2)}) %collective-permute-start) | collective-permute-done | bytes 532512 | tf_op jit(solution)/shard_map/while/body/eval_jaxpr/ppermute | solution.py:29
  207.7 9.9 %copy.83 = bf16[4,2,8,16,516]{3,0,1,2,4:T(4,128)(2,1)} copy(bf16[4,2,8,16,516]{4,3,2,1,0:T(8,128)(2,1)S(1)} %bitcast.86) | data formatting | bytes 2113536 | tf_op jit(solution)/shard_map/reshape | solution.py:80
  217.6 9.7 %gather_fusion.1 = bf16[8,4,2,16,256]{3,1,2,4,0:T(4,128)(2,1)} fusion(bf16[8,4,2,16,516]{3,1,2,0,4:T(4,128)(2,1)} %bitcast.82, s32[8]{0:T(128)S(1)} %copy-done.4), kind=kCustom, calls=%fused_computation.1 | custom fusion | bytes 1048736 | tf_op jit(solution)/shard_map/vmap()/gather | solution.py:90
  232.9 9.7 %gather_fusion.2 = bf16[8,4,2,16,256]{3,1,2,4,0:T(4,128)(2,1)} fusion(bf16[8,4,2,16,516]{3,1,2,0,4:T(4,128)(2,1)} %bitcast.83, s32[8]{0:T(128)S(1)} %get-tuple-element.390), kind=kCustom, calls=%fused_computation.2 | custom fusion | bytes 1048736 | tf_op jit(solution)/shard_map/vmap()/gather | solution.py:90
  248.2 9.7 %gather_fusion.3 = bf16[8,4,2,16,256]{3,1,2,4,0:T(4,128)(2,1)} fusion(bf16[8,4,2,16,516]{3,1,2,0,4:T(4,128)(2,1)} %bitcast.84, s32[8]{0:T(128)S(1)} %get-tuple-element.389), kind=kCustom, calls=%fused_computation.3 | custom fusion | bytes 1048736 | tf_op jit(solution)/shard_map/vmap()/gather | solution.py:90
  257.9 5.6 copy.87
  263.5 18.5 %gather_fusion = bf16[8,4,2,16,256]{3,1,2,4,0:T(4,128)(2,1)} fusion(bf16[8,4,2,16,516]{3,1,2,0,4:T(4,128)(2,1)} %bitcast.85, s32[8]{0:T(128)S(1)} %get-tuple-element.379), kind=kCustom, calls=%fused_computation | custom fusion | bytes 1048736 | tf_op jit(solution)/shard_map/vmap()/gather | solution.py:90
  288.4 11.0 %collective-permute-start.5 = (bf16[2,2,128,1]{3,2,1,0:T(8,128)(2,1)S(1)}, bf16[2,2,128,1]{3,2,1,0:T(8,128)(2,1)S(1)}, u32[]{:S(2)}, u32[]{:S(2)}) collective-permute-start(bf16[2,2,128,1]{3,2,1,0:T(8,128)(2,1)S(1)} %get-tuple-element.334), channel_id=1, source_target_pairs={{8,0},{16,8},{24,16},{32,24},{40,32},{48,40},{56,48},{64,56},{72,6... | collective-permute-start | bytes 3080 | tf_op jit(solution)/shard_map/ppermute | solution.py:21
  306.5 7.7 collective-permute-start.9
  321.0 7.0 collective-permute-start.13
  334.9 7.0 collective-permute-start.17
  349.2 7.0 collective-permute-start.21
  363.1 7.0 collective-permute-start.25
  377.0 7.0 collective-permute-start.29
  390.9 7.0 collective-permute-start.33
  404.7 7.0 collective-permute-start.37
  418.6 7.0 collective-permute-start.41
  432.6 7.0 collective-permute-start.45
  442.2 198.4 %while.37 = (s32[]{:T(128)}, bf16[4,2,128,260]{2,0,3,1:T(4,128)(2,1)S(1)}, bf16[4,2,128,260]{2,0,3,1:T(4,128)(2,1)S(1)}, bf16[4,2,128,260]{2,0,3,1:T(4,128)(2,1)S(1)}, s32[8]{0:T(128)S(1)}, /*index=5*/s32[]{:T(128)}) while((s32[]{:T(128)}, bf16[4,2,128,260]{2,0,3,1:T(4,128)(2,1)S(1)}, bf16[4,2,128,260]{2,0,3,1:T(4,128)(2,1)S(1)}, ...), condition=%wide.region_3.4_spmd.clone, body=%wide.region_2.3_spmd.clone.sunk | while | flops 532866 | bytes 5859993 | solution.py:76
  443.3 8.8 %collective-permute-done.1 = bf16[4,2,128,260]{2,0,3,1:T(4,128)(2,1)S(1)} collective-permute-done((bf16[4,2,128,260]{2,0,3,1:T(4,128)(2,1)S(1)}, bf16[4,2,128,260]{2,0,3,1:T(4,128)(2,1)S(1)}, u32[]{:S(2)}, u32[]{:S(2)}) %collective-permute-start.1) | collective-permute-done | bytes 532512 | tf_op jit(solution)/shard_map/while/body/eval_jaxpr/ppermute | solution.py:29
  453.7 10.9 %collective-permute-done.1 = bf16[4,2,128,260]{2,0,3,1:T(4,128)(2,1)S(1)} collective-permute-done((bf16[4,2,128,260]{2,0,3,1:T(4,128)(2,1)S(1)}, bf16[4,2,128,260]{2,0,3,1:T(4,128)(2,1)S(1)}, u32[]{:S(2)}, u32[]{:S(2)}) %collective-permute-start.1) | collective-permute-done | bytes 532512 | tf_op jit(solution)/shard_map/while/body/eval_jaxpr/ppermute | solution.py:29
  465.7 11.5 %collective-permute-done.1 = bf16[4,2,128,260]{2,0,3,1:T(4,128)(2,1)S(1)} collective-permute-done((bf16[4,2,128,260]{2,0,3,1:T(4,128)(2,1)S(1)}, bf16[4,2,128,260]{2,0,3,1:T(4,128)(2,1)S(1)}, u32[]{:S(2)}, u32[]{:S(2)}) %collective-permute-start.1) | collective-permute-done | bytes 532512 | tf_op jit(solution)/shard_map/while/body/eval_jaxpr/ppermute | solution.py:29
  478.2 11.5 %collective-permute-done.1 = bf16[4,2,128,260]{2,0,3,1:T(4,128)(2,1)S(1)} collective-permute-done((bf16[4,2,128,260]{2,0,3,1:T(4,128)(2,1)S(1)}, bf16[4,2,128,260]{2,0,3,1:T(4,128)(2,1)S(1)}, u32[]{:S(2)}, u32[]{:S(2)}) %collective-permute-start.1) | collective-permute-done | bytes 532512 | tf_op jit(solution)/shard_map/while/body/eval_jaxpr/ppermute | solution.py:29
  490.8 11.5 %collective-permute-done.1 = bf16[4,2,128,260]{2,0,3,1:T(4,128)(2,1)S(1)} collective-permute-done((bf16[4,2,128,260]{2,0,3,1:T(4,128)(2,1)S(1)}, bf16[4,2,128,260]{2,0,3,1:T(4,128)(2,1)S(1)}, u32[]{:S(2)}, u32[]{:S(2)}) %collective-permute-start.1) | collective-permute-done | bytes 532512 | tf_op jit(solution)/shard_map/while/body/eval_jaxpr/ppermute | solution.py:29
  503.4 11.5 %collective-permute-done.1 = bf16[4,2,128,260]{2,0,3,1:T(4,128)(2,1)S(1)} collective-permute-done((bf16[4,2,128,260]{2,0,3,1:T(4,128)(2,1)S(1)}, bf16[4,2,128,260]{2,0,3,1:T(4,128)(2,1)S(1)}, u32[]{:S(2)}, u32[]{:S(2)}) %collective-permute-start.1) | collective-permute-done | bytes 532512 | tf_op jit(solution)/shard_map/while/body/eval_jaxpr/ppermute | solution.py:29
  515.9 11.5 %collective-permute-done.1 = bf16[4,2,128,260]{2,0,3,1:T(4,128)(2,1)S(1)} collective-permute-done((bf16[4,2,128,260]{2,0,3,1:T(4,128)(2,1)S(1)}, bf16[4,2,128,260]{2,0,3,1:T(4,128)(2,1)S(1)}, u32[]{:S(2)}, u32[]{:S(2)}) %collective-permute-start.1) | collective-permute-done | bytes 532512 | tf_op jit(solution)/shard_map/while/body/eval_jaxpr/ppermute | solution.py:29
  528.5 11.5 %collective-permute-done.1 = bf16[4,2,128,260]{2,0,3,1:T(4,128)(2,1)S(1)} collective-permute-done((bf16[4,2,128,260]{2,0,3,1:T(4,128)(2,1)S(1)}, bf16[4,2,128,260]{2,0,3,1:T(4,128)(2,1)S(1)}, u32[]{:S(2)}, u32[]{:S(2)}) %collective-permute-start.1) | collective-permute-done | bytes 532512 | tf_op jit(solution)/shard_map/while/body/eval_jaxpr/ppermute | solution.py:29
  541.1 11.5 %collective-permute-done.1 = bf16[4,2,128,260]{2,0,3,1:T(4,128)(2,1)S(1)} collective-permute-done((bf16[4,2,128,260]{2,0,3,1:T(4,128)(2,1)S(1)}, bf16[4,2,128,260]{2,0,3,1:T(4,128)(2,1)S(1)}, u32[]{:S(2)}, u32[]{:S(2)}) %collective-permute-start.1) | collective-permute-done | bytes 532512 | tf_op jit(solution)/shard_map/while/body/eval_jaxpr/ppermute | solution.py:29
  553.6 11.5 %collective-permute-done.1 = bf16[4,2,128,260]{2,0,3,1:T(4,128)(2,1)S(1)} collective-permute-done((bf16[4,2,128,260]{2,0,3,1:T(4,128)(2,1)S(1)}, bf16[4,2,128,260]{2,0,3,1:T(4,128)(2,1)S(1)}, u32[]{:S(2)}, u32[]{:S(2)}) %collective-permute-start.1) | collective-permute-done | bytes 532512 | tf_op jit(solution)/shard_map/while/body/eval_jaxpr/ppermute | solution.py:29
  566.2 11.5 %collective-permute-done.1 = bf16[4,2,128,260]{2,0,3,1:T(4,128)(2,1)S(1)} collective-permute-done((bf16[4,2,128,260]{2,0,3,1:T(4,128)(2,1)S(1)}, bf16[4,2,128,260]{2,0,3,1:T(4,128)(2,1)S(1)}, u32[]{:S(2)}, u32[]{:S(2)}) %collective-permute-start.1) | collective-permute-done | bytes 532512 | tf_op jit(solution)/shard_map/while/body/eval_jaxpr/ppermute | solution.py:29
  578.8 11.5 %collective-permute-done.1 = bf16[4,2,128,260]{2,0,3,1:T(4,128)(2,1)S(1)} collective-permute-done((bf16[4,2,128,260]{2,0,3,1:T(4,128)(2,1)S(1)}, bf16[4,2,128,260]{2,0,3,1:T(4,128)(2,1)S(1)}, u32[]{:S(2)}, u32[]{:S(2)}) %collective-permute-start.1) | collective-permute-done | bytes 532512 | tf_op jit(solution)/shard_map/while/body/eval_jaxpr/ppermute | solution.py:29
  591.3 11.5 %collective-permute-done.1 = bf16[4,2,128,260]{2,0,3,1:T(4,128)(2,1)S(1)} collective-permute-done((bf16[4,2,128,260]{2,0,3,1:T(4,128)(2,1)S(1)}, bf16[4,2,128,260]{2,0,3,1:T(4,128)(2,1)S(1)}, u32[]{:S(2)}, u32[]{:S(2)}) %collective-permute-start.1) | collective-permute-done | bytes 532512 | tf_op jit(solution)/shard_map/while/body/eval_jaxpr/ppermute | solution.py:29
  603.9 11.5 %collective-permute-done.1 = bf16[4,2,128,260]{2,0,3,1:T(4,128)(2,1)S(1)} collective-permute-done((bf16[4,2,128,260]{2,0,3,1:T(4,128)(2,1)S(1)}, bf16[4,2,128,260]{2,0,3,1:T(4,128)(2,1)S(1)}, u32[]{:S(2)}, u32[]{:S(2)}) %collective-permute-start.1) | collective-permute-done | bytes 532512 | tf_op jit(solution)/shard_map/while/body/eval_jaxpr/ppermute | solution.py:29
  616.5 11.5 %collective-permute-done.1 = bf16[4,2,128,260]{2,0,3,1:T(4,128)(2,1)S(1)} collective-permute-done((bf16[4,2,128,260]{2,0,3,1:T(4,128)(2,1)S(1)}, bf16[4,2,128,260]{2,0,3,1:T(4,128)(2,1)S(1)}, u32[]{:S(2)}, u32[]{:S(2)}) %collective-permute-start.1) | collective-permute-done | bytes 532512 | tf_op jit(solution)/shard_map/while/body/eval_jaxpr/ppermute | solution.py:29
  629.0 11.5 %collective-permute-done.1 = bf16[4,2,128,260]{2,0,3,1:T(4,128)(2,1)S(1)} collective-permute-done((bf16[4,2,128,260]{2,0,3,1:T(4,128)(2,1)S(1)}, bf16[4,2,128,260]{2,0,3,1:T(4,128)(2,1)S(1)}, u32[]{:S(2)}, u32[]{:S(2)}) %collective-permute-start.1) | collective-permute-done | bytes 532512 | tf_op jit(solution)/shard_map/while/body/eval_jaxpr/ppermute | solution.py:29
  644.3 9.9 %copy.99 = bf16[4,2,8,16,516]{3,0,1,2,4:T(4,128)(2,1)} copy(bf16[4,2,8,16,516]{4,3,2,1,0:T(8,128)(2,1)S(1)} %bitcast.87) | data formatting | bytes 2113536 | tf_op jit(solution)/shard_map/reshape | solution.py:80
  654.2 9.7 %gather_fusion.5 = bf16[8,4,2,16,256]{3,1,2,4,0:T(4,128)(2,1)} fusion(bf16[8,4,2,16,516]{3,1,2,0,4:T(4,128)(2,1)} %bitcast.78, s32[8]{0:T(128)S(1)} %copy-done.3), kind=kCustom, calls=%fused_computation.5 | custom fusion | bytes 1048736 | tf_op jit(solution)/shard_map/vmap()/gather | solution.py:90
  669.5 9.7 %gather_fusion.6 = bf16[8,4,2,16,256]{3,1,2,4,0:T(4,128)(2,1)} fusion(bf16[8,4,2,16,516]{3,1,2,0,4:T(4,128)(2,1)} %bitcast.79, s32[8]{0:T(128)S(1)} %copy-done.2), kind=kCustom, calls=%fused_computation.6 | custom fusion | bytes 1048736 | tf_op jit(solution)/shard_map/vmap()/gather | solution.py:90
  679.2 5.6 copy.102
  684.9 9.7 %gather_fusion.4 = bf16[8,4,2,16,256]{3,1,2,4,0:T(4,128)(2,1)} fusion(bf16[8,4,2,16,516]{3,1,2,0,4:T(4,128)(2,1)} %bitcast.80, s32[8]{0:T(128)S(1)} %get-tuple-element.261), kind=kCustom, calls=%fused_computation.4 | custom fusion | bytes 1048736 | tf_op jit(solution)/shard_map/vmap()/gather | solution.py:90
  700.2 10.1 %gather_fusion.7 = bf16[8,4,2,16,256]{3,1,2,4,0:T(4,128)(2,1)} fusion(bf16[8,4,2,16,516]{3,1,2,0,4:T(4,128)(2,1)} %bitcast.81, s32[8]{0:T(128)S(1)} %copy-done.1), kind=kCustom, calls=%fused_computation.7 | custom fusion | bytes 1048736 | tf_op jit(solution)/shard_map/vmap()/gather | solution.py:90
  716.7 11.0 %collective-permute-start.47 = (bf16[2,2,128,1]{3,2,1,0:T(8,128)(2,1)S(1)}, bf16[2,2,128,1]{3,2,1,0:T(8,128)(2,1)S(1)}, u32[]{:S(2)}, u32[]{:S(2)}) collective-permute-start(bf16[2,2,128,1]{3,2,1,0:T(8,128)(2,1)S(1)} %get-tuple-element.312), channel_id=1, source_target_pairs={{8,0},{16,8},{24,16},{32,24},{40,32},{48,40},{56,48},{64,56},{72,6... | collective-permute-start | bytes 3080 | tf_op jit(solution)/shard_map/ppermute | solution.py:21
  735.1 7.6 collective-permute-start.51
  749.6 7.0 collective-permute-start.55
  763.5 7.0 collective-permute-start.59
  777.4 7.1 collective-permute-start.63
  791.4 7.0 collective-permute-start.67
  805.3 7.0 collective-permute-start.71
  819.2 7.0 collective-permute-start.75
  833.0 7.0 collective-permute-start.79
  846.9 7.0 collective-permute-start.83
  (499 shorter events, 265.7 us)
Async XLA Ops:
  1.3 9.5 %collective-permute-start.2 = (bf16[4,2,128,2]{2,0,3,1:T(4,128)(2,1)S(1)}, bf16[4,2,128,2]{2,0,3,1:T(4,128)(2,1)S(1)}, u32[]{:S(2)}, u32[]{:S(2)}) collective-permute-start(bf16[4,2,128,2]{2,0,3,1:T(4,128)(2,1)S(1)} %get-tuple-element.287), channel_id=1, source_target_pairs={{0,8},{8,16},{16,24},{24,32},{32,40},{40,48},{48,56},{56,64},{64,7... | collective-permute-start | bytes 12296 | tf_op jit(solution)/shard_map/ppermute | solution.py:20
  11.9 9.5 %collective-permute-start = (bf16[4,2,128,260]{2,0,3,1:T(4,128)(2,1)S(1)}, bf16[4,2,128,260]{2,0,3,1:T(4,128)(2,1)S(1)}, u32[]{:S(2)}, u32[]{:S(2)}) collective-permute-start(bf16[4,2,128,260]{2,0,3,1:T(4,128)(2,1)S(1)} %copy.114), channel_id=1, source_target_pairs={{0,8},{8,16},{16,24},{24,32},{32,40},{40,48},{48,56},{56,64},{64,7... | collective-permute-start | bytes 1597448 | tf_op jit(solution)/shard_map/while/body/eval_jaxpr/ppermute | solution.py:29
  21.6 10.3 %collective-permute-start = (bf16[4,2,128,260]{2,0,3,1:T(4,128)(2,1)S(1)}, bf16[4,2,128,260]{2,0,3,1:T(4,128)(2,1)S(1)}, u32[]{:S(2)}, u32[]{:S(2)}) collective-permute-start(bf16[4,2,128,260]{2,0,3,1:T(4,128)(2,1)S(1)} %copy.114), channel_id=1, source_target_pairs={{0,8},{8,16},{16,24},{24,32},{32,40},{40,48},{48,56},{56,64},{64,7... | collective-permute-start | bytes 1597448 | tf_op jit(solution)/shard_map/while/body/eval_jaxpr/ppermute | solution.py:29
  32.0 10.3 %collective-permute-start = (bf16[4,2,128,260]{2,0,3,1:T(4,128)(2,1)S(1)}, bf16[4,2,128,260]{2,0,3,1:T(4,128)(2,1)S(1)}, u32[]{:S(2)}, u32[]{:S(2)}) collective-permute-start(bf16[4,2,128,260]{2,0,3,1:T(4,128)(2,1)S(1)} %copy.114), channel_id=1, source_target_pairs={{0,8},{8,16},{16,24},{24,32},{32,40},{40,48},{48,56},{56,64},{64,7... | collective-permute-start | bytes 1597448 | tf_op jit(solution)/shard_map/while/body/eval_jaxpr/ppermute | solution.py:29
  42.5 10.7 %collective-permute-start = (bf16[4,2,128,260]{2,0,3,1:T(4,128)(2,1)S(1)}, bf16[4,2,128,260]{2,0,3,1:T(4,128)(2,1)S(1)}, u32[]{:S(2)}, u32[]{:S(2)}) collective-permute-start(bf16[4,2,128,260]{2,0,3,1:T(4,128)(2,1)S(1)} %copy.114), channel_id=1, source_target_pairs={{0,8},{8,16},{16,24},{24,32},{32,40},{40,48},{48,56},{56,64},{64,7... | collective-permute-start | bytes 1597448 | tf_op jit(solution)/shard_map/while/body/eval_jaxpr/ppermute | solution.py:29
  53.3 12.4 %collective-permute-start = (bf16[4,2,128,260]{2,0,3,1:T(4,128)(2,1)S(1)}, bf16[4,2,128,260]{2,0,3,1:T(4,128)(2,1)S(1)}, u32[]{:S(2)}, u32[]{:S(2)}) collective-permute-start(bf16[4,2,128,260]{2,0,3,1:T(4,128)(2,1)S(1)} %copy.114), channel_id=1, source_target_pairs={{0,8},{8,16},{16,24},{24,32},{32,40},{40,48},{48,56},{56,64},{64,7... | collective-permute-start | bytes 1597448 | tf_op jit(solution)/shard_map/while/body/eval_jaxpr/ppermute | solution.py:29
  65.9 12.4 %collective-permute-start = (bf16[4,2,128,260]{2,0,3,1:T(4,128)(2,1)S(1)}, bf16[4,2,128,260]{2,0,3,1:T(4,128)(2,1)S(1)}, u32[]{:S(2)}, u32[]{:S(2)}) collective-permute-start(bf16[4,2,128,260]{2,0,3,1:T(4,128)(2,1)S(1)} %copy.114), channel_id=1, source_target_pairs={{0,8},{8,16},{16,24},{24,32},{32,40},{40,48},{48,56},{56,64},{64,7... | collective-permute-start | bytes 1597448 | tf_op jit(solution)/shard_map/while/body/eval_jaxpr/ppermute | solution.py:29
  78.5 12.4 %collective-permute-start = (bf16[4,2,128,260]{2,0,3,1:T(4,128)(2,1)S(1)}, bf16[4,2,128,260]{2,0,3,1:T(4,128)(2,1)S(1)}, u32[]{:S(2)}, u32[]{:S(2)}) collective-permute-start(bf16[4,2,128,260]{2,0,3,1:T(4,128)(2,1)S(1)} %copy.114), channel_id=1, source_target_pairs={{0,8},{8,16},{16,24},{24,32},{32,40},{40,48},{48,56},{56,64},{64,7... | collective-permute-start | bytes 1597448 | tf_op jit(solution)/shard_map/while/body/eval_jaxpr/ppermute | solution.py:29
  91.0 12.4 %collective-permute-start = (bf16[4,2,128,260]{2,0,3,1:T(4,128)(2,1)S(1)}, bf16[4,2,128,260]{2,0,3,1:T(4,128)(2,1)S(1)}, u32[]{:S(2)}, u32[]{:S(2)}) collective-permute-start(bf16[4,2,128,260]{2,0,3,1:T(4,128)(2,1)S(1)} %copy.114), channel_id=1, source_target_pairs={{0,8},{8,16},{16,24},{24,32},{32,40},{40,48},{48,56},{56,64},{64,7... | collective-permute-start | bytes 1597448 | tf_op jit(solution)/shard_map/while/body/eval_jaxpr/ppermute | solution.py:29
  103.6 12.4 %collective-permute-start = (bf16[4,2,128,260]{2,0,3,1:T(4,128)(2,1)S(1)}, bf16[4,2,128,260]{2,0,3,1:T(4,128)(2,1)S(1)}, u32[]{:S(2)}, u32[]{:S(2)}) collective-permute-start(bf16[4,2,128,260]{2,0,3,1:T(4,128)(2,1)S(1)} %copy.114), channel_id=1, source_target_pairs={{0,8},{8,16},{16,24},{24,32},{32,40},{40,48},{48,56},{56,64},{64,7... | collective-permute-start | bytes 1597448 | tf_op jit(solution)/shard_map/while/body/eval_jaxpr/ppermute | solution.py:29
  116.2 12.4 %collective-permute-start = (bf16[4,2,128,260]{2,0,3,1:T(4,128)(2,1)S(1)}, bf16[4,2,128,260]{2,0,3,1:T(4,128)(2,1)S(1)}, u32[]{:S(2)}, u32[]{:S(2)}) collective-permute-start(bf16[4,2,128,260]{2,0,3,1:T(4,128)(2,1)S(1)} %copy.114), channel_id=1, source_target_pairs={{0,8},{8,16},{16,24},{24,32},{32,40},{40,48},{48,56},{56,64},{64,7... | collective-permute-start | bytes 1597448 | tf_op jit(solution)/shard_map/while/body/eval_jaxpr/ppermute | solution.py:29
  128.7 12.4 %collective-permute-start = (bf16[4,2,128,260]{2,0,3,1:T(4,128)(2,1)S(1)}, bf16[4,2,128,260]{2,0,3,1:T(4,128)(2,1)S(1)}, u32[]{:S(2)}, u32[]{:S(2)}) collective-permute-start(bf16[4,2,128,260]{2,0,3,1:T(4,128)(2,1)S(1)} %copy.114), channel_id=1, source_target_pairs={{0,8},{8,16},{16,24},{24,32},{32,40},{40,48},{48,56},{56,64},{64,7... | collective-permute-start | bytes 1597448 | tf_op jit(solution)/shard_map/while/body/eval_jaxpr/ppermute | solution.py:29
  141.3 12.4 %collective-permute-start = (bf16[4,2,128,260]{2,0,3,1:T(4,128)(2,1)S(1)}, bf16[4,2,128,260]{2,0,3,1:T(4,128)(2,1)S(1)}, u32[]{:S(2)}, u32[]{:S(2)}) collective-permute-start(bf16[4,2,128,260]{2,0,3,1:T(4,128)(2,1)S(1)} %copy.114), channel_id=1, source_target_pairs={{0,8},{8,16},{16,24},{24,32},{32,40},{40,48},{48,56},{56,64},{64,7... | collective-permute-start | bytes 1597448 | tf_op jit(solution)/shard_map/while/body/eval_jaxpr/ppermute | solution.py:29
  153.9 12.4 %collective-permute-start = (bf16[4,2,128,260]{2,0,3,1:T(4,128)(2,1)S(1)}, bf16[4,2,128,260]{2,0,3,1:T(4,128)(2,1)S(1)}, u32[]{:S(2)}, u32[]{:S(2)}) collective-permute-start(bf16[4,2,128,260]{2,0,3,1:T(4,128)(2,1)S(1)} %copy.114), channel_id=1, source_target_pairs={{0,8},{8,16},{16,24},{24,32},{32,40},{40,48},{48,56},{56,64},{64,7... | collective-permute-start | bytes 1597448 | tf_op jit(solution)/shard_map/while/body/eval_jaxpr/ppermute | solution.py:29
  166.4 12.4 %collective-permute-start = (bf16[4,2,128,260]{2,0,3,1:T(4,128)(2,1)S(1)}, bf16[4,2,128,260]{2,0,3,1:T(4,128)(2,1)S(1)}, u32[]{:S(2)}, u32[]{:S(2)}) collective-permute-start(bf16[4,2,128,260]{2,0,3,1:T(4,128)(2,1)S(1)} %copy.114), channel_id=1, source_target_pairs={{0,8},{8,16},{16,24},{24,32},{32,40},{40,48},{48,56},{56,64},{64,7... | collective-permute-start | bytes 1597448 | tf_op jit(solution)/shard_map/while/body/eval_jaxpr/ppermute | solution.py:29
  179.0 12.4 %collective-permute-start = (bf16[4,2,128,260]{2,0,3,1:T(4,128)(2,1)S(1)}, bf16[4,2,128,260]{2,0,3,1:T(4,128)(2,1)S(1)}, u32[]{:S(2)}, u32[]{:S(2)}) collective-permute-start(bf16[4,2,128,260]{2,0,3,1:T(4,128)(2,1)S(1)} %copy.114), channel_id=1, source_target_pairs={{0,8},{8,16},{16,24},{24,32},{32,40},{40,48},{48,56},{56,64},{64,7... | collective-permute-start | bytes 1597448 | tf_op jit(solution)/shard_map/while/body/eval_jaxpr/ppermute | solution.py:29
  191.6 12.4 %collective-permute-start = (bf16[4,2,128,260]{2,0,3,1:T(4,128)(2,1)S(1)}, bf16[4,2,128,260]{2,0,3,1:T(4,128)(2,1)S(1)}, u32[]{:S(2)}, u32[]{:S(2)}) collective-permute-start(bf16[4,2,128,260]{2,0,3,1:T(4,128)(2,1)S(1)} %copy.114), channel_id=1, source_target_pairs={{0,8},{8,16},{16,24},{24,32},{32,40},{40,48},{48,56},{56,64},{64,7... | collective-permute-start | bytes 1597448 | tf_op jit(solution)/shard_map/while/body/eval_jaxpr/ppermute | solution.py:29
  288.4 11.8 %collective-permute-start.4 = (bf16[2,2,128,1]{3,2,1,0:T(8,128)(2,1)S(1)}, bf16[2,2,128,1]{3,2,1,0:T(8,128)(2,1)S(1)}, u32[]{:S(2)}, u32[]{:S(2)}) collective-permute-start(bf16[2,2,128,1]{3,2,1,0:T(8,128)(2,1)S(1)} %get-tuple-element.333), channel_id=1, source_target_pairs={{0,8},{8,16},{16,24},{24,32},{32,40},{40,48},{48,56},{56,64},{64,7... | collective-permute-start | bytes 3080 | tf_op jit(solution)/shard_map/ppermute | solution.py:20
  288.4 11.9 %collective-permute-start.5 = (bf16[2,2,128,1]{3,2,1,0:T(8,128)(2,1)S(1)}, bf16[2,2,128,1]{3,2,1,0:T(8,128)(2,1)S(1)}, u32[]{:S(2)}, u32[]{:S(2)}) collective-permute-start(bf16[2,2,128,1]{3,2,1,0:T(8,128)(2,1)S(1)} %get-tuple-element.334), channel_id=1, source_target_pairs={{8,0},{16,8},{24,16},{32,24},{40,32},{48,40},{56,48},{64,56},{72,6... | collective-permute-start | bytes 3080 | tf_op jit(solution)/shard_map/ppermute | solution.py:21
  306.4 8.4 collective-permute-start.8
  306.5 8.6 collective-permute-start.9
  320.9 7.8 collective-permute-start.12
  321.0 7.9 collective-permute-start.13
  334.9 7.9 collective-permute-start.17
  348.7 8.1 collective-permute-start.20
  349.2 7.9 collective-permute-start.21
  363.0 7.7 collective-permute-start.24
  363.1 7.9 collective-permute-start.25
  376.9 7.7 collective-permute-start.28
  377.0 7.9 collective-permute-start.29
  390.9 7.9 collective-permute-start.33
  404.7 7.9 collective-permute-start.37
  418.6 7.9 collective-permute-start.41
  432.6 8.0 collective-permute-start.44
  432.6 8.1 collective-permute-start.45
  442.4 9.7 %collective-permute-start.1 = (bf16[4,2,128,260]{2,0,3,1:T(4,128)(2,1)S(1)}, bf16[4,2,128,260]{2,0,3,1:T(4,128)(2,1)S(1)}, u32[]{:S(2)}, u32[]{:S(2)}) collective-permute-start(bf16[4,2,128,260]{2,0,3,1:T(4,128)(2,1)S(1)} %copy.126), channel_id=1, source_target_pairs={{0,8},{8,16},{16,24},{24,32},{32,40},{40,48},{48,56},{56,64},{64,7... | collective-permute-start | bytes 1597448 | tf_op jit(solution)/shard_map/while/body/eval_jaxpr/ppermute | solution.py:29
  452.3 12.4 %collective-permute-start.1 = (bf16[4,2,128,260]{2,0,3,1:T(4,128)(2,1)S(1)}, bf16[4,2,128,260]{2,0,3,1:T(4,128)(2,1)S(1)}, u32[]{:S(2)}, u32[]{:S(2)}) collective-permute-start(bf16[4,2,128,260]{2,0,3,1:T(4,128)(2,1)S(1)} %copy.126), channel_id=1, source_target_pairs={{0,8},{8,16},{16,24},{24,32},{32,40},{40,48},{48,56},{56,64},{64,7... | collective-permute-start | bytes 1597448 | tf_op jit(solution)/shard_map/while/body/eval_jaxpr/ppermute | solution.py:29
  464.8 12.4 %collective-permute-start.1 = (bf16[4,2,128,260]{2,0,3,1:T(4,128)(2,1)S(1)}, bf16[4,2,128,260]{2,0,3,1:T(4,128)(2,1)S(1)}, u32[]{:S(2)}, u32[]{:S(2)}) collective-permute-start(bf16[4,2,128,260]{2,0,3,1:T(4,128)(2,1)S(1)} %copy.126), channel_id=1, source_target_pairs={{0,8},{8,16},{16,24},{24,32},{32,40},{40,48},{48,56},{56,64},{64,7... | collective-permute-start | bytes 1597448 | tf_op jit(solution)/shard_map/while/body/eval_jaxpr/ppermute | solution.py:29
  477.4 12.4 %collective-permute-start.1 = (bf16[4,2,128,260]{2,0,3,1:T(4,128)(2,1)S(1)}, bf16[4,2,128,260]{2,0,3,1:T(4,128)(2,1)S(1)}, u32[]{:S(2)}, u32[]{:S(2)}) collective-permute-start(bf16[4,2,128,260]{2,0,3,1:T(4,128)(2,1)S(1)} %copy.126), channel_id=1, source_target_pairs={{0,8},{8,16},{16,24},{24,32},{32,40},{40,48},{48,56},{56,64},{64,7... | collective-permute-start | bytes 1597448 | tf_op jit(solution)/shard_map/while/body/eval_jaxpr/ppermute | solution.py:29
  490.0 12.4 %collective-permute-start.1 = (bf16[4,2,128,260]{2,0,3,1:T(4,128)(2,1)S(1)}, bf16[4,2,128,260]{2,0,3,1:T(4,128)(2,1)S(1)}, u32[]{:S(2)}, u32[]{:S(2)}) collective-permute-start(bf16[4,2,128,260]{2,0,3,1:T(4,128)(2,1)S(1)} %copy.126), channel_id=1, source_target_pairs={{0,8},{8,16},{16,24},{24,32},{32,40},{40,48},{48,56},{56,64},{64,7... | collective-permute-start | bytes 1597448 | tf_op jit(solution)/shard_map/while/body/eval_jaxpr/ppermute | solution.py:29
  502.5 12.4 %collective-permute-start.1 = (bf16[4,2,128,260]{2,0,3,1:T(4,128)(2,1)S(1)}, bf16[4,2,128,260]{2,0,3,1:T(4,128)(2,1)S(1)}, u32[]{:S(2)}, u32[]{:S(2)}) collective-permute-start(bf16[4,2,128,260]{2,0,3,1:T(4,128)(2,1)S(1)} %copy.126), channel_id=1, source_target_pairs={{0,8},{8,16},{16,24},{24,32},{32,40},{40,48},{48,56},{56,64},{64,7... | collective-permute-start | bytes 1597448 | tf_op jit(solution)/shard_map/while/body/eval_jaxpr/ppermute | solution.py:29
  515.1 12.4 %collective-permute-start.1 = (bf16[4,2,128,260]{2,0,3,1:T(4,128)(2,1)S(1)}, bf16[4,2,128,260]{2,0,3,1:T(4,128)(2,1)S(1)}, u32[]{:S(2)}, u32[]{:S(2)}) collective-permute-start(bf16[4,2,128,260]{2,0,3,1:T(4,128)(2,1)S(1)} %copy.126), channel_id=1, source_target_pairs={{0,8},{8,16},{16,24},{24,32},{32,40},{40,48},{48,56},{56,64},{64,7... | collective-permute-start | bytes 1597448 | tf_op jit(solution)/shard_map/while/body/eval_jaxpr/ppermute | solution.py:29
  527.7 12.4 %collective-permute-start.1 = (bf16[4,2,128,260]{2,0,3,1:T(4,128)(2,1)S(1)}, bf16[4,2,128,260]{2,0,3,1:T(4,128)(2,1)S(1)}, u32[]{:S(2)}, u32[]{:S(2)}) collective-permute-start(bf16[4,2,128,260]{2,0,3,1:T(4,128)(2,1)S(1)} %copy.126), channel_id=1, source_target_pairs={{0,8},{8,16},{16,24},{24,32},{32,40},{40,48},{48,56},{56,64},{64,7... | collective-permute-start | bytes 1597448 | tf_op jit(solution)/shard_map/while/body/eval_jaxpr/ppermute | solution.py:29
  540.2 12.4 %collective-permute-start.1 = (bf16[4,2,128,260]{2,0,3,1:T(4,128)(2,1)S(1)}, bf16[4,2,128,260]{2,0,3,1:T(4,128)(2,1)S(1)}, u32[]{:S(2)}, u32[]{:S(2)}) collective-permute-start(bf16[4,2,128,260]{2,0,3,1:T(4,128)(2,1)S(1)} %copy.126), channel_id=1, source_target_pairs={{0,8},{8,16},{16,24},{24,32},{32,40},{40,48},{48,56},{56,64},{64,7... | collective-permute-start | bytes 1597448 | tf_op jit(solution)/shard_map/while/body/eval_jaxpr/ppermute | solution.py:29
  552.8 12.4 %collective-permute-start.1 = (bf16[4,2,128,260]{2,0,3,1:T(4,128)(2,1)S(1)}, bf16[4,2,128,260]{2,0,3,1:T(4,128)(2,1)S(1)}, u32[]{:S(2)}, u32[]{:S(2)}) collective-permute-start(bf16[4,2,128,260]{2,0,3,1:T(4,128)(2,1)S(1)} %copy.126), channel_id=1, source_target_pairs={{0,8},{8,16},{16,24},{24,32},{32,40},{40,48},{48,56},{56,64},{64,7... | collective-permute-start | bytes 1597448 | tf_op jit(solution)/shard_map/while/body/eval_jaxpr/ppermute | solution.py:29
  565.4 12.4 %collective-permute-start.1 = (bf16[4,2,128,260]{2,0,3,1:T(4,128)(2,1)S(1)}, bf16[4,2,128,260]{2,0,3,1:T(4,128)(2,1)S(1)}, u32[]{:S(2)}, u32[]{:S(2)}) collective-permute-start(bf16[4,2,128,260]{2,0,3,1:T(4,128)(2,1)S(1)} %copy.126), channel_id=1, source_target_pairs={{0,8},{8,16},{16,24},{24,32},{32,40},{40,48},{48,56},{56,64},{64,7... | collective-permute-start | bytes 1597448 | tf_op jit(solution)/shard_map/while/body/eval_jaxpr/ppermute | solution.py:29
  577.9 12.4 %collective-permute-start.1 = (bf16[4,2,128,260]{2,0,3,1:T(4,128)(2,1)S(1)}, bf16[4,2,128,260]{2,0,3,1:T(4,128)(2,1)S(1)}, u32[]{:S(2)}, u32[]{:S(2)}) collective-permute-start(bf16[4,2,128,260]{2,0,3,1:T(4,128)(2,1)S(1)} %copy.126), channel_id=1, source_target_pairs={{0,8},{8,16},{16,24},{24,32},{32,40},{40,48},{48,56},{56,64},{64,7... | collective-permute-start | bytes 1597448 | tf_op jit(solution)/shard_map/while/body/eval_jaxpr/ppermute | solution.py:29
  590.5 12.4 %collective-permute-start.1 = (bf16[4,2,128,260]{2,0,3,1:T(4,128)(2,1)S(1)}, bf16[4,2,128,260]{2,0,3,1:T(4,128)(2,1)S(1)}, u32[]{:S(2)}, u32[]{:S(2)}) collective-permute-start(bf16[4,2,128,260]{2,0,3,1:T(4,128)(2,1)S(1)} %copy.126), channel_id=1, source_target_pairs={{0,8},{8,16},{16,24},{24,32},{32,40},{40,48},{48,56},{56,64},{64,7... | collective-permute-start | bytes 1597448 | tf_op jit(solution)/shard_map/while/body/eval_jaxpr/ppermute | solution.py:29
  603.1 12.4 %collective-permute-start.1 = (bf16[4,2,128,260]{2,0,3,1:T(4,128)(2,1)S(1)}, bf16[4,2,128,260]{2,0,3,1:T(4,128)(2,1)S(1)}, u32[]{:S(2)}, u32[]{:S(2)}) collective-permute-start(bf16[4,2,128,260]{2,0,3,1:T(4,128)(2,1)S(1)} %copy.126), channel_id=1, source_target_pairs={{0,8},{8,16},{16,24},{24,32},{32,40},{40,48},{48,56},{56,64},{64,7... | collective-permute-start | bytes 1597448 | tf_op jit(solution)/shard_map/while/body/eval_jaxpr/ppermute | solution.py:29
  615.6 12.4 %collective-permute-start.1 = (bf16[4,2,128,260]{2,0,3,1:T(4,128)(2,1)S(1)}, bf16[4,2,128,260]{2,0,3,1:T(4,128)(2,1)S(1)}, u32[]{:S(2)}, u32[]{:S(2)}) collective-permute-start(bf16[4,2,128,260]{2,0,3,1:T(4,128)(2,1)S(1)} %copy.126), channel_id=1, source_target_pairs={{0,8},{8,16},{16,24},{24,32},{32,40},{40,48},{48,56},{56,64},{64,7... | collective-permute-start | bytes 1597448 | tf_op jit(solution)/shard_map/while/body/eval_jaxpr/ppermute | solution.py:29
  628.2 12.4 %collective-permute-start.1 = (bf16[4,2,128,260]{2,0,3,1:T(4,128)(2,1)S(1)}, bf16[4,2,128,260]{2,0,3,1:T(4,128)(2,1)S(1)}, u32[]{:S(2)}, u32[]{:S(2)}) collective-permute-start(bf16[4,2,128,260]{2,0,3,1:T(4,128)(2,1)S(1)} %copy.126), channel_id=1, source_target_pairs={{0,8},{8,16},{16,24},{24,32},{32,40},{40,48},{48,56},{56,64},{64,7... | collective-permute-start | bytes 1597448 | tf_op jit(solution)/shard_map/while/body/eval_jaxpr/ppermute | solution.py:29
  716.6 11.8 %collective-permute-start.46 = (bf16[2,2,128,1]{3,2,1,0:T(8,128)(2,1)S(1)}, bf16[2,2,128,1]{3,2,1,0:T(8,128)(2,1)S(1)}, u32[]{:S(2)}, u32[]{:S(2)}) collective-permute-start(bf16[2,2,128,1]{3,2,1,0:T(8,128)(2,1)S(1)} %get-tuple-element.311), channel_id=1, source_target_pairs={{0,8},{8,16},{16,24},{24,32},{32,40},{40,48},{48,56},{56,64},{64,7... | collective-permute-start | bytes 3080 | tf_op jit(solution)/shard_map/ppermute | solution.py:20
  716.7 11.9 %collective-permute-start.47 = (bf16[2,2,128,1]{3,2,1,0:T(8,128)(2,1)S(1)}, bf16[2,2,128,1]{3,2,1,0:T(8,128)(2,1)S(1)}, u32[]{:S(2)}, u32[]{:S(2)}) collective-permute-start(bf16[2,2,128,1]{3,2,1,0:T(8,128)(2,1)S(1)} %get-tuple-element.312), channel_id=1, source_target_pairs={{8,0},{16,8},{24,16},{32,24},{40,32},{48,40},{56,48},{64,56},{72,6... | collective-permute-start | bytes 3080 | tf_op jit(solution)/shard_map/ppermute | solution.py:21
  735.0 8.3 collective-permute-start.50
  735.1 8.5 collective-permute-start.51
  749.5 7.8 collective-permute-start.54
  749.6 7.9 collective-permute-start.55
  763.5 7.9 collective-permute-start.59
  777.4 8.0 collective-permute-start.63
  791.4 7.9 collective-permute-start.67
  805.3 7.9 collective-permute-start.71
  819.2 7.9 collective-permute-start.75
  833.0 7.9 collective-permute-start.79
  846.9 7.9 collective-permute-start.83
  (60 other events, 456.1 us)
where the time goes:
time: 877 us; the launch traced here: 862 us
  waiting for transfers between devices  380 us (43%)
  starting transfers between devices  268 us (31%)
  local copies, waits for them, and re-layouts  173 us (20%)
  other arithmetic  39.2 us (4%)
    ppermute x32, waiting for transfers between devices, shifted(): return lax.ppermute(value, axis, pairs)  337 us
    ppermute x42, starting transfers between devices, with_halo(): after = lax.ppermute(first, axis, down)  229 us
    gather x16, local copies, waits for them, and re-layouts, interp_block(): lax.dynamic_slice_in_dim(window_part, cell_count + 3 - node_index - block...  132 us
    ppermute x42, waiting for transfers between devices, with_halo(): before = lax.ppermute(last, axis, up)  37.5 us
    ppermute x32, starting transfers between devices, shifted(): return lax.ppermute(value, axis, pairs)  23.2 us
    reshape x2, local copies, waits for them, and re-layouts, upstream_rows(): window.reshape(window.shape[0], window.shape[1], block_count, block_rows,...  19.8 us
    select_n x32, other arithmetic, cycle_step(): far_tile = jnp.where(pick_far, moving, far_tile)  18.9 us
  transfers between devices with their start and end apart: 116, of which 95 were waited for; matrix products, arithmetic and copies ran while one was open for 3% of the time, Pallas kernels for 0%

commit v1 on v0

v1 whole, which is shorter than its diff:
```python
import functools

import jax
import jax.numpy as jnp
from jax import lax
from jax.experimental import pallas as pl
from jax.experimental.pallas import tpu as pltpu
from jax.sharding import PartitionSpec as P

STEPS = 2
SWEEPS = 8
ROWS = 16
LANES = 128
GROUP = 8
F32 = jnp.float32
BF16 = jnp.bfloat16
MESH = pl.DeviceIdType.MESH


def place_of(lon):
    return 2 * (lon // 4) + lon % 2, (lon // 2) % 2


def lon_of(block, level):
    return 4 * (block // 2) + 2 * level + block % 2


def cubic_weights(a):
    am, ap, a2 = a - 1.0, a + 1.0, a - 2.0
    left, right = a * am, ap * a2
    return (
        left * a2 * (-1.0 / 6.0),
        right * am * 0.5,
        right * a * -0.5,
        ap * left * (1.0 / 6.0),
    )


def kernel(
    n_lon, n_lat, fields, shifts, fractions, helm, out,
    x, frac, field, adv, res, src, scaled, pot, down, up, above, below,
    in_send, in_recv, halo_send, halo_recv, out_send, out_recv,
):
    n_cols = n_lon * fields.shape[3]
    tile = fields.shape[3]
    n_chunks = n_cols // LANES
    n_blocks = fields.shape[2] // ROWS
    lon, lat = lax.axis_index("lon"), lax.axis_index("lat")
    block, level = place_of(lon)

    prev_block = lax.rem(block + n_blocks - 1, n_blocks)
    next_block = lax.rem(block + 1, n_blocks)
    lat_up = lax.rem(lat + n_lat - (block == 0).astype(jnp.int32), n_lat)
    lat_down = lax.rem(lat + (block == n_blocks - 1).astype(jnp.int32), n_lat)
    dev_up = {"lon": lon_of(prev_block, level), "lat": lat_up}
    dev_down = {"lon": lon_of(next_block, level), "lat": lat_down}
    row_block = lat * n_blocks + block
    has_above = row_block > 0
    has_below = row_block < n_lat * n_blocks - 1

    def rows_of(b):
        return pl.ds(pl.multiple_of(b * ROWS, ROWS), ROWS)

    def cols_of(p):
        return pl.ds(pl.multiple_of(p * tile, tile), tile)

    def chunk(k):
        return pl.ds(pl.multiple_of(k * LANES, LANES), LANES)

    barrier = pltpu.get_barrier_semaphore()

    def greet(j, _):
        peer = lax.rem(lon + j, n_lon)
        pl.semaphore_signal(barrier, inc=1, device_id={"lon": peer, "lat": lat}, device_id_type=MESH)
        return 0

    lax.fori_loop(1, n_lon, greet, 0)
    pl.semaphore_signal(barrier, inc=1, device_id=dev_up, device_id_type=MESH)
    pl.semaphore_signal(barrier, inc=1, device_id=dev_down, device_id_type=MESH)
    pl.semaphore_wait(barrier, n_lon + 1)

    def in_refs(part, to_block, to_level, from_lon):
        if part == 0:
            return (fields.at[0:3, to_level, rows_of(to_block), :], x.at[0:3, :, cols_of(from_lon)])
        if part == 2:
            return (fields.at[3, to_level, rows_of(to_block), :], x.at[3, :, cols_of(from_lon)])
        step = part // 2
        return (fractions.at[step, rows_of(to_block), :], frac.at[step, :, cols_of(from_lon)])

    def send_parts(parts):
        def turn(j, _):
            peer = lax.rem(lon + j, n_lon)
            to_block, to_level = place_of(peer)
            for part in parts:
                from_ref, to_ref = in_refs(part, to_block, to_level, lon)
                pltpu.make_async_remote_copy(
                    src_ref=from_ref,
                    dst_ref=to_ref,
                    send_sem=in_send.at[part],
                    recv_sem=in_recv.at[part],
                    device_id={"lon": peer, "lat": lat},
                    device_id_type=MESH,
                ).start()
            return 0

        lax.fori_loop(1, n_lon, turn, 0)
        for part in parts:
            from_ref, to_ref = in_refs(part, block, level, lon)
            pltpu.make_async_copy(from_ref, to_ref, in_recv.at[part]).start()

    def in_whole(part):
        return (x.at[0:3], frac.at[0], x.at[3], frac.at[1])[part]

    def wait_in(part):
        whole = in_whole(part)
        pltpu.make_async_copy(whole, whole, in_recv.at[part]).wait()

    def wait_in_sent(part):
        whole = in_whole(part)
        sent = whole.at[:, :, 0 : n_cols - tile] if part == 0 else whole.at[:, 0 : n_cols - tile]
        pltpu.make_async_copy(sent, sent, in_send.at[part]).wait()

    send_parts((0, 1))
    send_parts((2, 3))

    lane = lax.broadcasted_iota(jnp.int32, (ROWS, LANES), 1)
    row16 = lax.broadcasted_iota(jnp.int32, (ROWS, LANES), 0)
    lane32 = lax.broadcasted_iota(jnp.int32, (2 * ROWS, LANES), 1)
    row32 = lax.broadcasted_iota(jnp.int32, (2 * ROWS, LANES), 0)

    coef = jnp.full((2 * ROWS, LANES), helm[level], F32)
    inverse = 1.0 / (1.0 + 4.0 * coef)
    inside = ((row32 >= 8) | has_above) & ((row32 < 24) | has_below)
    weight = jnp.where(inside, coef * inverse, 0.0)

    def unpack(parts):
        def turn(g, _):
            for j in range(GROUP):
                k = g * GROUP + j
                for f in parts:
                    field[f, k] = x[f, :, chunk(k)].astype(F32)
            return 0

        lax.fori_loop(0, n_chunks // GROUP, turn, 0)

    def advect(step, sources, targets):
        shift = shifts[step, block]
        taps = []
        for d in (1, 0, -1, -2):
            total = lax.rem(shift + (n_cols - d), n_cols)
            taps.append((lax.div(total, LANES), lax.rem(total, LANES)))
        from_here = [lane >= part for _, part in taps]

        def rolled(f, k, tap):
            whole, part = taps[tap]
            at = lax.rem(k - whole + 2 * n_chunks, n_chunks)
            return pltpu.roll(field[f, at], part, 1)

        first = tuple(rolled(f, -1, tap) for f in sources for tap in range(4))

        def turn(k, before):
            w = cubic_weights(frac[step, :, chunk(k)])
            now = []
            for f, to in zip(sources, targets):
                total = None
                for tap in range(4):
                    here = rolled(f, k, tap)
                    value = jnp.where(from_here[tap], here, before[len(now)])
                    now.append(here)
                    total = w[tap] * value if total is None else total + w[tap] * value
                to(k, total.astype(BF16))
            return tuple(now)

        lax.fori_loop(0, n_chunks, turn, first, unroll=2)

    def around(g, load):
        base = g * GROUP
        vals = [load(lax.rem(base + j + n_chunks, n_chunks)) for j in range(-1, GROUP + 1)]
        return vals

    def east_west(vals, ln):
        east = [None] + [pltpu.roll(v, LANES - 1, 1) for v in vals[1:]]
        west = [pltpu.roll(v, 1, 1) for v in vals[:-1]]
        last, first = ln == LANES - 1, ln == 0
        return [
            (
                jnp.where(last, east[j + 1], east[j]),
                jnp.where(first, west[j - 1], west[j]),
            )
            for j in range(1, len(vals) - 1)
        ]

    def sources(step):
        def turn(g, _):
            wind = around(g, lambda k: adv[1, :, chunk(k)].astype(F32))
            for j, (e, w) in enumerate(east_west(wind, lane)):
                k = g * GROUP + j
                north = adv[2, :, chunk(k)].astype(F32)
                after = jnp.where(row16 == ROWS - 1, 0.0, pltpu.roll(north, ROWS - 1, 0))
                prior = jnp.where(row16 == 0, 0.0, pltpu.roll(north, 1, 0))
                own = adv[0, :, chunk(k)].astype(F32) - 0.25 * ((e - w) + (after - prior))
                src[ROWS : 2 * ROWS, chunk(k)] = own
                turned = pltpu.roll(north, 1, 0)
                down[step, :, chunk(k)] = jnp.where(row16 == 0, turned, own).astype(BF16)
                turned = pltpu.roll(north, ROWS - 1, 0)
                up[step, :, chunk(k)] = jnp.where(row16 == ROWS - 1, turned, own).astype(BF16)
            return 0

        lax.fori_loop(0, n_chunks // GROUP, turn, 0)

    def halo_copies(step):
        return (
            pltpu.make_async_remote_copy(
                src_ref=down.at[step],
                dst_ref=above.at[step],
                send_sem=halo_send.at[step, 0],
                recv_sem=halo_recv.at[step, 0],
                device_id=dev_down,
                device_id_type=MESH,
            ),
            pltpu.make_async_remote_copy(
                src_ref=up.at[step],
                dst_ref=below.at[step],
                send_sem=halo_send.at[step, 1],
                recv_sem=halo_recv.at[step, 1],
                device_id=dev_up,
                device_id_type=MESH,
            ),
        )

    def complete(step):
        def turn(g, _):
            for j in range(GROUP):
                k = g * GROUP + j
                north = adv[2, :, chunk(k)].astype(F32)
                own = src[ROWS : 2 * ROWS, chunk(k)]
                a = jnp.where(has_above, above[step, :, chunk(k)].astype(F32), 0.0)
                b = jnp.where(has_below, below[step, :, chunk(k)].astype(F32), 0.0)
                own = own + 0.25 * jnp.where(row16 == 0, a, 0.0)
                own = own - 0.25 * jnp.where(row16 == ROWS - 1, b, 0.0)
                to_a = jnp.where((row16 == ROWS - 1) & has_above, pltpu.roll(north, ROWS - 1, 0), 0.0)
                to_b = jnp.where((row16 == 0) & has_below, pltpu.roll(north, 1, 0), 0.0)
                src[0:ROWS, chunk(k)] = a - 0.25 * to_a
                src[ROWS : 2 * ROWS, chunk(k)] = own
                src[2 * ROWS : 3 * ROWS, chunk(k)] = b + 0.25 * to_b
            return 0

        lax.fori_loop(0, n_chunks // GROUP, turn, 0)

    def first_sweep():
        def turn(g, _):
            vals = around(g, lambda k: src[8:40, chunk(k)])
            for j, (e, w) in enumerate(east_west(vals, lane32)):
                k = g * GROUP + j
                column = src[:, chunk(k)]
                n = pltpu.roll(column, 1, 0)[8:40]
                s = pltpu.roll(column, 3 * ROWS - 1, 0)[8:40]
                fixed = vals[j + 1] * inverse
                scaled[:, chunk(k)] = fixed
                pot[0, :, chunk(k)] = fixed + weight * ((e + w) + (n + s))
            return 0

        lax.fori_loop(0, n_chunks // GROUP, turn, 0)

    def later_sweeps():
        def sweep(i, _):
            now, then = lax.rem(i, 2), lax.rem(i + 1, 2)

            def turn(g, _):
                vals = around(g, lambda k: pot[now, :, chunk(k)])
                for j, (e, w) in enumerate(east_west(vals, lane32)):
                    k = g * GROUP + j
                    n = pltpu.roll(vals[j + 1], 1, 0)
                    s = pltpu.roll(vals[j + 1], 2 * ROWS - 1, 0)
                    pot[then, :, chunk(k)] = scaled[:, chunk(k)] + weight * ((e + w) + (n + s))
                return 0

            lax.fori_loop(0, n_chunks // GROUP, turn, 0)
            return 0

        lax.fori_loop(0, SWEEPS - 1, sweep, 0)

    solved = (SWEEPS - 1) % 2

    def update(k, e, w, column, to):
        n = pltpu.roll(column, 1, 0)[8:24]
        s = pltpu.roll(column, 2 * ROWS - 1, 0)[8:24]
        to(0, k, column[8:24].astype(BF16))
        to(1, k, (adv[1, :, chunk(k)].astype(F32) - 0.25 * (e - w)).astype(BF16))
        to(2, k, (adv[2, :, chunk(k)].astype(F32) - 0.25 * (s - n)).astype(BF16))

    def to_field(f, k, value):
        field[f, k] = value.astype(F32)

    def to_res(f, k, value):
        res[f, :, chunk(k)] = value

    def to_adv(f, k, value):
        adv[f, :, chunk(k)] = value

    def update_all():
        def turn(g, _):
            vals = around(g, lambda k: pot[solved, 8:24, chunk(k)])
            for j, (e, w) in enumerate(east_west(vals, lane)):
                k = g * GROUP + j
                update(k, e, w, pot[solved, :, chunk(k)], to_field)
            return 0

        lax.fori_loop(0, n_chunks // GROUP, turn, 0)

    def out_copy(part, peer):
        fs = slice(0, 3) if part == 0 else slice(3, 4)
        return pltpu.make_async_remote_copy(
            src_ref=res.at[fs, :, cols_of(peer)],
            dst_ref=out.at[fs, level, rows_of(block), :],
            send_sem=out_send.at[part],
            recv_sem=out_recv,
            device_id={"lon": peer, "lat": lat},
            device_id_type=MESH,
        )

    def out_keep(part):
        fs = slice(0, 3) if part == 0 else slice(3, 4)
        return pltpu.make_async_copy(
            res.at[fs, :, cols_of(lon)], out.at[fs, level, rows_of(block), :], out_recv
        )

    def update_and_send():
        per = tile // LANES

        def turn(j, _):
            peer = lax.rem(lon + j, n_lon)
            base = peer * per
            at = [lax.rem(base + i + n_chunks, n_chunks) for i in range(-1, per + 1)]
            vals = [pot[solved, 8:24, chunk(k)] for k in at]
            for i, (e, w) in enumerate(east_west(vals, lane)):
                k = base + i
                update(k, e, w, pot[solved, :, chunk(k)], to_res)

            @pl.when(j < n_lon)
            def _():
                out_copy(0, peer).start()

            return 0

        lax.fori_loop(1, n_lon + 1, turn, 0)
        out_keep(0).start()

    for step in range(STEPS):
        last = step == STEPS - 1
        if step == 0:
            wait_in(0)
            wait_in(1)
            unpack((0, 1, 2))
        else:
            wait_in(3)
        advect(step, range(3), [functools.partial(to_adv, f) for f in range(3)])
        sources(step)
        copies = halo_copies(step)
        for c in copies:
            c.start()
        if step == 0:
            wait_in(2)
            unpack((3,))
        advect(step, [3 + step], [functools.partial(to_res if last else to_field, 3 + (not last))])
        if last:

            def send_res3(j, _):
                out_copy(1, lax.rem(lon + j, n_lon)).start()
                return 0

            lax.fori_loop(1, n_lon, send_res3, 0)
            out_keep(1).start()
        for c in copies:
            c.wait_recv()
        complete(step)
        first_sweep()
        later_sweeps()
        if last:
            update_and_send()
        else:
            update_all()

    for part in range(4):
        wait_in_sent(part)
    for step in range(STEPS):
        for c in halo_copies(step):
            c.wait_send()
    sent = res.at[0:3, :, 0 : n_cols - tile]
    pltpu.make_async_copy(sent, sent, out_send.at[0]).wait()
    sent = res.at[3:4, :, 0 : n_cols - tile]
    pltpu.make_async_copy(sent, sent, out_send.at[1]).wait()
    pltpu.make_async_copy(out, out, out_recv).wait()


def local(n_lon, n_lat, fields, shifts, fractions, helm_coef):
    n_cols = n_lon * fields.shape[3]
    return pl.pallas_call(
        functools.partial(kernel, n_lon, n_lat),
        out_shape=jax.ShapeDtypeStruct(fields.shape, BF16),
        in_specs=[
            pl.BlockSpec(memory_space=pl.ANY),
            pl.BlockSpec(memory_space=pltpu.SMEM),
            pl.BlockSpec(memory_space=pl.ANY),
            pl.BlockSpec(memory_space=pltpu.SMEM),
        ],
        out_specs=pl.BlockSpec(memory_space=pl.ANY),
        scratch_shapes=[
            pltpu.VMEM((4, ROWS, n_cols), BF16),
            pltpu.VMEM((STEPS, ROWS, n_cols), F32),
            pltpu.VMEM((5, n_cols // LANES, ROWS, LANES), F32),
            pltpu.VMEM((3, ROWS, n_cols), BF16),
            pltpu.VMEM((4, ROWS, n_cols), BF16),
            pltpu.VMEM((3 * ROWS, n_cols), F32),
            pltpu.VMEM((2 * ROWS, n_cols), F32),
            pltpu.VMEM((2, 2 * ROWS, n_cols), F32),
            pltpu.VMEM((STEPS, ROWS, n_cols), BF16),
            pltpu.VMEM((STEPS, ROWS, n_cols), BF16),
            pltpu.VMEM((STEPS, ROWS, n_cols), BF16),
            pltpu.VMEM((STEPS, ROWS, n_cols), BF16),
            pltpu.SemaphoreType.DMA((4,)),
            pltpu.SemaphoreType.DMA((4,)),
            pltpu.SemaphoreType.DMA((STEPS, 2)),
            pltpu.SemaphoreType.DMA((STEPS, 2)),
            pltpu.SemaphoreType.DMA((2,)),
            pltpu.SemaphoreType.DMA,
        ],
        compiler_params=pltpu.CompilerParams(
            collective_id=0, has_side_effects=True, vmem_limit_bytes=32 * 2**20
        ),
        name="transport",
    )(fields, shifts, fractions, helm_coef)


def solution(mesh):
    return jax.shard_map(
        functools.partial(local, mesh.shape["lon"], mesh.shape["lat"]),
        mesh=mesh,
        in_specs=(P(None, None, "lat", "lon"), P(None, "lat"), P(None, "lat", "lon"), P()),
        out_specs=P(None, None, "lat", "lon"),
        check_vma=False,
    )
```

time: 877 us -> 56.5 us (0.06); the launches traced: 862 us -> 56.3 us
  waiting for transfers between devices: 380 us -> 0 us
  starting transfers between devices: 268 us -> 0 us
  local copies, waits for them, and re-layouts: 173 us -> 4.12 us
  Pallas kernels: 0 us -> 52.2 us
  other arithmetic: 39.2 us -> 0 us
    ppermute x116 -> x0, waiting for transfers between devices: 380 us -> none  [the longest x32 337 us: shifted(): return lax.ppermute(value, axis, pairs)]
    ppermute x116 -> x0, starting transfers between devices: 268 us -> none  [the longest x42 229 us: with_halo(): after = lax.ppermute(first, axis, down)]
    gather x16 -> x0, local copies, waits for them, and re-layouts: 132 us -> none  [interp_block(): lax.dynamic_slice_in_dim(window_part, cell_count + 3 - node_index - block...]
    pallas_call x0 -> x1, Pallas kernels: none -> 52.2 us  [local(): pl.pallas_call(functools.partial(kernel, n_lon, n_lat), out_shape=jax.Sha...]
    select_n x35 -> x0, other arithmetic: 22.5 us -> none  [the longest x32 18.9 us: cycle_step(): far_tile = jnp.where(pick_far, moving, far_tile)]
    reshape x36 -> x0, local copies, waits for them, and re-layouts: 22.5 us -> none  [the longest x2 19.8 us: upstream_rows(): window.reshape(window.shape[0], window.shape[1], block_count, block_rows,...]
    while x38 -> x0, local copies, waits for them, and re-layouts: 10.7 us -> none
  transfers between devices with their start and end apart: 116 -> 0, of which waited for: 95 -> 0; matrix products, arithmetic and copies ran while one was open for 3% -> 0% of each run, Pallas kernels for 0% -> 0%
where the time goes in v1:
time: 56.5 us; the launch traced here: 56.3 us
  Pallas kernels  52.2 us (92%)
  local copies, waits for them, and re-layouts  4.12 us (7%)
    pallas_call x1, Pallas kernels, local(): pl.pallas_call(functools.partial(kernel, n_lon, n_lat), out_shape=jax.Sha...  52.2 us
    unnamed x9, local copies, waits for them, and re-layouts  4.12 us

profile of v1, /device:TPU:1, one launch (start us, length us, event | category | flops | bytes accessed | tf_op | source)
XLA Modules:
  0.0 56.3 jit_solution(9953860620908382784)
XLA Ops:
  0.0 0.0 copy-start
  0.0 1.0 %copy-done = bf16[4,2,128,256]{3,2,1,0:T(8,128)(2,1)S(1)} copy-done((bf16[4,2,128,256]{3,2,1,0:T(8,128)(2,1)S(1)}, bf16[4,2,128,256]{3,2,1,0:T(8,128)(2,1)}, u32[]{:S(2)}) %copy-start) | copy-done | bytes 524312
  1.0 0.0 copy-start.1
  1.0 0.9 %copy-done.1 = f32[2,128,256]{2,1,0:T(8,128)S(1)} copy-done((f32[2,128,256]{2,1,0:T(8,128)S(1)}, f32[2,128,256]{2,1,0:T(8,128)}, u32[]{:S(2)}) %copy-start.1) | copy-done | bytes 262168
  2.0 0.0 copy-start.2
  2.0 0.7 %copy-done.2 = s32[2,8]{1,0:T(2,128)S(1)} copy-done((s32[2,8]{1,0:T(2,128)S(1)}, s32[2,8]{1,0:T(2,128)}, u32[]{:S(2)}) %copy-start.2) | copy-done | bytes 88
  2.7 0.0 copy-start.3
  2.7 0.7 %copy-done.3 = f32[2]{0:T(128)S(1)} copy-done((f32[2]{0:T(128)S(1)}, f32[2]{0:T(128)}, u32[]{:S(2)}) %copy-start.3) | copy-done | bytes 32
  3.3 52.2 %transport.1 = bf16[4,2,128,256]{3,2,1,0:T(8,128)(2,1)S(1)} custom-call(bf16[4,2,128,256]{3,2,1,0:T(8,128)(2,1)S(1)} %copy-done, s32[2,8]{1,0:T(2,128)S(1)} %copy-done.2, f32[2,128,256]{2,1,0:T(8,128)S(1)} %copy-done.1, f32[2]{0:T(128)S(1)} %copy-done.3), custom_call_target="tpu_custom_call" | custom-call | tf_op jit(solution)/shard_map/transport/pallas_call | solution.py:398
  55.5 0.8 %copy.6 = bf16[4,2,128,256]{3,2,1,0:T(8,128)(2,1)} copy(bf16[4,2,128,256]{3,2,1,0:T(8,128)(2,1)S(1)} %transport.1) | data formatting | bytes 1048576
Async XLA Ops:
  0.0 1.0 %copy-start = (bf16[4,2,128,256]{3,2,1,0:T(8,128)(2,1)S(1)}, bf16[4,2,128,256]{3,2,1,0:T(8,128)(2,1)}, u32[]{:S(2)}) copy-start(bf16[4,2,128,256]{3,2,1,0:T(8,128)(2,1)} %fields.1) | copy-start | bytes 1572868
  1.0 0.9 %copy-start.1 = (f32[2,128,256]{2,1,0:T(8,128)S(1)}, f32[2,128,256]{2,1,0:T(8,128)}, u32[]{:S(2)}) copy-start(f32[2,128,256]{2,1,0:T(8,128)} %fractions.1) | copy-start | bytes 786436
  2.0 0.7 %copy-start.2 = (s32[2,8]{1,0:T(2,128)S(1)}, s32[2,8]{1,0:T(2,128)}, u32[]{:S(2)}) copy-start(s32[2,8]{1,0:T(2,128)} %shifts.1) | copy-start | bytes 196
  2.7 0.7 %copy-start.3 = (f32[2]{0:T(128)S(1)}, f32[2]{0:T(128)}, u32[]{:S(2)}) copy-start(f32[2]{0:T(128)} %helm.1) | copy-start | bytes 28

commit v2 on v1

v2 whole, which is shorter than its diff:
```python
import functools

import jax
import jax.numpy as jnp
from jax import lax
from jax.experimental import pallas as pl
from jax.experimental.pallas import tpu as pltpu
from jax.sharding import PartitionSpec as P

STEPS = 2
SWEEPS = 8
ROWS = 16
LANES = 128
GROUP = 16
F32 = jnp.float32
BF16 = jnp.bfloat16
MESH = pl.DeviceIdType.MESH


def place_of(lon):
    return 2 * (lon // 4) + lon % 2, (lon // 2) % 2


def lon_of(block, level):
    return 4 * (block // 2) + 2 * level + block % 2


def cubic_weights(a):
    am, ap, a2 = a - 1.0, a + 1.0, a - 2.0
    left, right = a * am, ap * a2
    return (
        left * a2 * (-1.0 / 6.0),
        right * am * 0.5,
        right * a * -0.5,
        ap * left * (1.0 / 6.0),
    )


def kernel(
    n_lon, n_lat, fields, shifts_hbm, fractions, helm_hbm, out,
    shifts, helm, x, frac, field, adv, north, res, src, scaled, pot, down, up, above, below,
    small, in_send, in_recv, halo_send, halo_recv, out_send, out_recv,
):
    n_cols = n_lon * fields.shape[3]
    tile = fields.shape[3]
    n_chunks = n_cols // LANES
    n_blocks = fields.shape[2] // ROWS
    lon, lat = lax.axis_index("lon"), lax.axis_index("lat")
    block, level = place_of(lon)

    prev_block = lax.rem(block + n_blocks - 1, n_blocks)
    next_block = lax.rem(block + 1, n_blocks)
    lat_up = lax.rem(lat + n_lat - (block == 0).astype(jnp.int32), n_lat)
    lat_down = lax.rem(lat + (block == n_blocks - 1).astype(jnp.int32), n_lat)
    dev_up = {"lon": lon_of(prev_block, level), "lat": lat_up}
    dev_down = {"lon": lon_of(next_block, level), "lat": lat_down}
    row_block = lat * n_blocks + block
    has_above = row_block > 0
    has_below = row_block < n_lat * n_blocks - 1

    def rows_of(b):
        return pl.ds(pl.multiple_of(b * ROWS, ROWS), ROWS)

    def cols_of(p):
        return pl.ds(pl.multiple_of(p * tile, tile), tile)

    def chunk(k):
        return pl.ds(pl.multiple_of(k * LANES, LANES), LANES)

    def wrap(k):
        return k & (n_chunks - 1)

    def each_group(turn):
        def body(g, _):
            turn(g * GROUP)
            return 0

        lax.fori_loop(0, n_chunks // GROUP, body, 0)

    barrier = pltpu.get_barrier_semaphore()

    def greet(j, _):
        peer = lax.rem(lon + j, n_lon)
        pl.semaphore_signal(barrier, inc=1, device_id={"lon": peer, "lat": lat}, device_id_type=MESH)
        return 0

    lax.fori_loop(1, n_lon, greet, 0)
    pl.semaphore_signal(barrier, inc=1, device_id=dev_up, device_id_type=MESH)
    pl.semaphore_signal(barrier, inc=1, device_id=dev_down, device_id_type=MESH)

    get_shifts = pltpu.make_async_copy(shifts_hbm, shifts, small.at[0])
    get_helm = pltpu.make_async_copy(helm_hbm, helm, small.at[1])
    get_shifts.start()
    get_helm.start()

    zero = jnp.zeros((8, LANES), F32)

    def clear(base):
        for j in range(GROUP):
            k = base + j
            north[k, 0:8] = zero
            north[k, 24:32] = zero
            for i in range(2):
                pot[i, k, 0:8] = zero
                pot[i, k, 40:48] = zero

    each_group(clear)
    pl.semaphore_wait(barrier, n_lon + 1)

    def in_refs(part, to_block, to_level, from_lon):
        if part == 0:
            return (fields.at[0:3, to_level, rows_of(to_block), :], x.at[0:3, :, cols_of(from_lon)])
        if part == 2:
            return (fields.at[3, to_level, rows_of(to_block), :], x.at[3, :, cols_of(from_lon)])
        step = part // 2
        return (fractions.at[step, rows_of(to_block), :], frac.at[step, :, cols_of(from_lon)])

    def send_parts(parts):
        def turn(j, _):
            peer = lax.rem(lon + j, n_lon)
            to_block, to_level = place_of(peer)
            for part in parts:
                from_ref, to_ref = in_refs(part, to_block, to_level, lon)
                pltpu.make_async_remote_copy(
                    src_ref=from_ref,
                    dst_ref=to_ref,
                    send_sem=in_send.at[part],
                    recv_sem=in_recv.at[part],
                    device_id={"lon": peer, "lat": lat},
                    device_id_type=MESH,
                ).start()
            return 0

        lax.fori_loop(1, n_lon, turn, 0)
        for part in parts:
            from_ref, to_ref = in_refs(part, block, level, lon)
            pltpu.make_async_copy(from_ref, to_ref, in_recv.at[part]).start()

    def in_whole(part):
        return (x.at[0:3], frac.at[0], x.at[3], frac.at[1])[part]

    def wait_in(part):
        whole = in_whole(part)
        pltpu.make_async_copy(whole, whole, in_recv.at[part]).wait()

    def wait_in_sent(part):
        whole = in_whole(part)
        sent = whole.at[:, :, 0 : n_cols - tile] if part == 0 else whole.at[:, 0 : n_cols - tile]
        pltpu.make_async_copy(sent, sent, in_send.at[part]).wait()

    send_parts((0, 1))
    send_parts((2, 3))
    get_shifts.wait()
    get_helm.wait()

    lane16 = lax.broadcasted_iota(jnp.int32, (ROWS, LANES), 1)
    row8 = lax.broadcasted_iota(jnp.int32, (8, LANES), 0)

    def weight_of(start, rows):
        row = start + lax.broadcasted_iota(jnp.int32, (rows, LANES), 0)
        coef = jnp.full((rows, LANES), helm[level], F32)
        inverse = 1.0 / (1.0 + 4.0 * coef)
        inside = ((row >= ROWS) | has_above) & ((row < 2 * ROWS) | has_below)
        return jnp.where(inside, coef * inverse, 0.0), inverse

    def unpack(parts):
        def turn(base):
            for j in range(GROUP):
                for f in parts:
                    field[f, base + j] = x[f, :, chunk(base + j)].astype(F32)

        each_group(turn)

    def advect(step, sources, targets):
        shift = shifts[step, block]
        taps = []
        for d in (1, 0, -1, -2):
            total = (shift + (n_cols - d)) & (n_cols - 1)
            taps.append((total // LANES, total & (LANES - 1)))
        from_here = [lane16 >= part for _, part in taps]

        def turn(base):
            weights = [cubic_weights(frac[step, :, chunk(base + j)]) for j in range(GROUP)]
            for f, to in zip(sources, targets):
                total = [None] * GROUP
                for tap, (whole, part) in enumerate(taps):
                    before = None
                    for j in range(-1, GROUP):
                        here = pltpu.roll(field[f, wrap(base + j - whole + n_chunks)], part, 1)
                        if j >= 0:
                            term = weights[j][tap] * jnp.where(from_here[tap], here, before)
                            total[j] = term if tap == 0 else total[j] + term
                        before = here
                for j in range(GROUP):
                    to(base + j, total[j].astype(BF16))

        each_group(turn)

    def east_west(base, count, load):
        vals = [load(wrap(base - 1 + n_chunks))] + [load(base + j) for j in range(count)]
        vals.append(load(wrap(base + count)))
        ln = lax.broadcasted_iota(jnp.int32, vals[0].shape, 1)
        last, first = ln == LANES - 1, ln == 0
        east = [None] + [pltpu.roll(v, LANES - 1, 1) for v in vals[1:]]
        west = [pltpu.roll(v, 1, 1) for v in vals[:-1]]
        return [
            (vals[j], jnp.where(last, east[j + 1], east[j]), jnp.where(first, west[j - 1], west[j]))
            for j in range(1, count + 1)
        ]

    def sources(step):
        def turn(base):
            for j, (_, e, w) in enumerate(east_west(base, GROUP, lambda k: adv[1, k])):
                k = base + j
                own = adv[0, k] - 0.25 * ((e - w) + (north[k, 9:25] - north[k, 7:23]))
                src[k, ROWS : 2 * ROWS] = own
                top, bottom = own[0:8], own[8:16]
                with_last = jnp.where(row8 == 0, north[k, 23:31], top)
                with_first = jnp.where(row8 == 7, north[k, 1:9], bottom)
                down[step, k] = jnp.concatenate([with_last, bottom], axis=0).astype(BF16)
                up[step, k] = jnp.concatenate([top, with_first], axis=0).astype(BF16)

        each_group(turn)

    def halo_copies(step):
        return (
            pltpu.make_async_remote_copy(
                src_ref=down.at[step],
                dst_ref=above.at[step],
                send_sem=halo_send.at[step, 0],
                recv_sem=halo_recv.at[step, 0],
                device_id=dev_down,
                device_id_type=MESH,
            ),
            pltpu.make_async_remote_copy(
                src_ref=up.at[step],
                dst_ref=below.at[step],
                send_sem=halo_send.at[step, 1],
                recv_sem=halo_recv.at[step, 1],
                device_id=dev_up,
                device_id_type=MESH,
            ),
        )

    def complete(step):
        first_has, last_has = (row8 == 0) & has_below, (row8 == 7) & has_above

        def turn(base):
            for j in range(GROUP):
                k = base + j
                a = jnp.where(has_above, above[step, k].astype(F32), 0.0)
                b = jnp.where(has_below, below[step, k].astype(F32), 0.0)
                src[k, 0:8] = a[0:8]
                src[k, 8:16] = a[8:16] - jnp.where(last_has, 0.25 * north[k, 1:9], 0.0)
                src[k, 16:24] = src[k, 16:24] + jnp.where(row8 == 0, 0.25 * a[0:8], 0.0)
                src[k, 24:32] = src[k, 24:32] - jnp.where(row8 == 7, 0.25 * b[8:16], 0.0)
                src[k, 32:40] = b[0:8] + jnp.where(first_has, 0.25 * north[k, 23:31], 0.0)
                src[k, 40:48] = b[8:16]

        each_group(turn)

    def first_sweep():
        weight, inverse = weight_of(8, 2 * ROWS)

        def turn(base):
            for j, (mid, e, w) in enumerate(east_west(base, GROUP, lambda k: src[k, 8:40])):
                k = base + j
                fixed = mid * inverse
                scaled[k] = fixed
                pot[0, k, 8:40] = fixed + weight * ((e + w) + (src[k, 7:39] + src[k, 9:41]))

        each_group(turn)

    def later_sweeps(begin, end, start, rows):
        weight, _ = weight_of(start, rows)

        def sweep(i, _):
            now, then = i & 1, (i + 1) & 1

            def turn(base):
                for j, (_, e, w) in enumerate(
                    east_west(base, GROUP, lambda k: pot[now, k, start : start + rows])
                ):
                    k = base + j
                    n = pot[now, k, start - 1 : start - 1 + rows]
                    s = pot[now, k, start + 1 : start + 1 + rows]
                    fixed = scaled[k, start - 8 : start - 8 + rows]
                    pot[then, k, start : start + rows] = fixed + weight * ((e + w) + (n + s))

            each_group(turn)
            return 0

        lax.fori_loop(begin, end, sweep, 0)

    solved = (SWEEPS - 1) % 2

    def update(base, count, to):
        own = east_west(base, count, lambda k: pot[solved, k, ROWS : 2 * ROWS])
        for j, (mid, e, w) in enumerate(own):
            k = base + j
            n, s = pot[solved, k, ROWS - 1 : 2 * ROWS - 1], pot[solved, k, ROWS + 1 : 2 * ROWS + 1]
            to(0, k, mid.astype(BF16))
            to(1, k, (adv[1, k] - 0.25 * (e - w)).astype(BF16))
            to(2, k, (north[k, 8:24] - 0.25 * (s - n)).astype(BF16))

    def to_field(f, k, value):
        field[f, k] = value.astype(F32)

    def to_res(f, k, value):
        res[f, :, chunk(k)] = value

    def to_adv(f, k, value):
        if f == 2:
            north[k, 8:24] = value.astype(F32)
        else:
            adv[f, k] = value.astype(F32)

    def out_copy(part, peer):
        fs = slice(0, 3) if part == 0 else slice(3, 4)
        return pltpu.make_async_remote_copy(
            src_ref=res.at[fs, :, cols_of(peer)],
            dst_ref=out.at[fs, level, rows_of(block), :],
            send_sem=out_send.at[part],
            recv_sem=out_recv,
            device_id={"lon": peer, "lat": lat},
            device_id_type=MESH,
        )

    def out_keep(part):
        fs = slice(0, 3) if part == 0 else slice(3, 4)
        return pltpu.make_async_copy(
            res.at[fs, :, cols_of(lon)], out.at[fs, level, rows_of(block), :], out_recv
        )

    def update_and_send():
        per = tile // LANES

        def turn(j, _):
            peer = lax.rem(lon + j, n_lon)
            update(peer * per, per, to_res)

            @pl.when(j < n_lon)
            def _():
                out_copy(0, peer).start()

            return 0

        lax.fori_loop(1, n_lon + 1, turn, 0)
        out_keep(0).start()

    for step in range(STEPS):
        last = step == STEPS - 1
        if step == 0:
            wait_in(0)
            wait_in(1)
            unpack((0, 1, 2))
        else:
            wait_in(3)
        advect(step, range(3), [functools.partial(to_adv, f) for f in range(3)])
        sources(step)
        copies = halo_copies(step)
        for c in copies:
            c.start()
        if step == 0:
            wait_in(2)
            unpack((3,))
        advect(step, [3 + step], [functools.partial(to_res if last else to_field, 3 + (not last))])
        if last:

            def send_res3(j, _):
                out_copy(1, lax.rem(lon + j, n_lon)).start()
                return 0

            lax.fori_loop(1, n_lon, send_res3, 0)
            out_keep(1).start()
        for c in copies:
            c.wait_recv()
        complete(step)
        first_sweep()
        later_sweeps(0, 3, 8, 32)
        later_sweeps(3, SWEEPS - 1, 12, 24)
        if last:
            update_and_send()
        else:
            each_group(lambda base: update(base, GROUP, to_field))

    for part in range(4):
        wait_in_sent(part)
    for step in range(STEPS):
        for c in halo_copies(step):
            c.wait_send()
    sent = res.at[0:3, :, 0 : n_cols - tile]
    pltpu.make_async_copy(sent, sent, out_send.at[0]).wait()
    sent = res.at[3:4, :, 0 : n_cols - tile]
    pltpu.make_async_copy(sent, sent, out_send.at[1]).wait()
    pltpu.make_async_copy(out, out, out_recv).wait()


def local(n_lon, n_lat, fields, shifts, fractions, helm_coef):
    n_cols = n_lon * fields.shape[3]
    n_chunks = n_cols // LANES
    return pl.pallas_call(
        functools.partial(kernel, n_lon, n_lat),
        out_shape=jax.ShapeDtypeStruct(fields.shape, BF16),
        in_specs=[pl.BlockSpec(memory_space=pltpu.HBM)] * 4,
        out_specs=pl.BlockSpec(memory_space=pl.ANY),
        scratch_shapes=[
            pltpu.SMEM(shifts.shape, jnp.int32),
            pltpu.SMEM(helm_coef.shape, F32),
            pltpu.VMEM((4, ROWS, n_cols), BF16),
            pltpu.VMEM((STEPS, ROWS, n_cols), F32),
            pltpu.VMEM((5, n_chunks, ROWS, LANES), F32),
            pltpu.VMEM((2, n_chunks, ROWS, LANES), F32),
            pltpu.VMEM((n_chunks, 2 * ROWS, LANES), F32),
            pltpu.VMEM((4, ROWS, n_cols), BF16),
            pltpu.VMEM((n_chunks, 3 * ROWS, LANES), F32),
            pltpu.VMEM((n_chunks, 2 * ROWS, LANES), F32),
            pltpu.VMEM((2, n_chunks, 3 * ROWS, LANES), F32),
            pltpu.VMEM((STEPS, n_chunks, ROWS, LANES), BF16),
            pltpu.VMEM((STEPS, n_chunks, ROWS, LANES), BF16),
            pltpu.VMEM((STEPS, n_chunks, ROWS, LANES), BF16),
            pltpu.VMEM((STEPS, n_chunks, ROWS, LANES), BF16),
            pltpu.SemaphoreType.DMA((2,)),
            pltpu.SemaphoreType.DMA((4,)),
            pltpu.SemaphoreType.DMA((4,)),
            pltpu.SemaphoreType.DMA((STEPS, 2)),
            pltpu.SemaphoreType.DMA((STEPS, 2)),
            pltpu.SemaphoreType.DMA((2,)),
            pltpu.SemaphoreType.DMA,
        ],
        compiler_params=pltpu.CompilerParams(
            collective_id=0, has_side_effects=True, vmem_limit_bytes=32 * 2**20
        ),
        name="transport",
    )(*[pltpu.with_memory_space_constraint(a, pltpu.HBM) for a in (fields, shifts, fractions, helm_coef)])


def solution(mesh):
    return jax.shard_map(
        functools.partial(local, mesh.shape["lon"], mesh.shape["lat"]),
        mesh=mesh,
        in_specs=(P(None, None, "lat", "lon"), P(None, "lat"), P(None, "lat", "lon"), P()),
        out_specs=P(None, None, "lat", "lon"),
        check_vma=False,
    )
```

time: 56.5 us -> 46.7 us (0.83)
  Pallas kernels: 52.2 us -> 45.8 us
  local copies, waits for them, and re-layouts: 4.12 us -> 0.8 us
    pallas_call x1, Pallas kernels: 52.2 us -> 45.8 us  [local(): pl.pallas_call(functools.partial(kernel, n_lon, n_lat), out_shape=jax.Sha...]
    unnamed x9 -> x1, local copies, waits for them, and re-layouts: 4.12 us -> 0.8 us
where the time goes in v2:
time: 46.7 us; the launch traced here: 46.6 us
  Pallas kernels  45.8 us (98%)
  local copies, waits for them, and re-layouts  0.8 us (2%)
    pallas_call x1, Pallas kernels, local(): pl.pallas_call(functools.partial(kernel, n_lon, n_lat), out_shape=jax.Sha...  45.8 us

profile of v2, /device:TPU:1, one launch (start us, length us, event | category | flops | bytes accessed | tf_op | source)
XLA Modules:
  0.0 46.6 jit_solution(2336388637557704398)
XLA Ops:
  0.0 45.8 %transport.1 = bf16[4,2,128,256]{3,2,1,0:T(8,128)(2,1)S(1)} custom-call(bf16[4,2,128,256]{3,2,1,0:T(8,128)(2,1)} %fields.1, s32[2,8]{1,0:T(2,128)} %shifts_hbm.1, f32[2,128,256]{2,1,0:T(8,128)} %fractions.1, f32[2]{0:T(128)} %helm_hbm.1), custom_call_target="tpu_custom_call" | custom-call | tf_op jit(solution)/shard_map/transport/pallas_call | solution.py:402
  45.8 0.8 %copy.6 = bf16[4,2,128,256]{3,2,1,0:T(8,128)(2,1)} copy(bf16[4,2,128,256]{3,2,1,0:T(8,128)(2,1)S(1)} %transport.1) | data formatting | bytes 1048576

commit v3 on v2

--- a/solution.py
+++ b/solution.py
@@ -11,9 +11,9 @@
 SWEEPS = 8
 ROWS = 16
 LANES = 128
-GROUP = 16
 F32 = jnp.float32
 BF16 = jnp.bfloat16
+UNITS, HALF = 65535.0, 32768
 MESH = pl.DeviceIdType.MESH
 
 
@@ -38,7 +38,7 @@
 
 def kernel(
     n_lon, n_lat, fields, shifts_hbm, fractions, helm_hbm, out,
-    shifts, helm, x, frac, field, adv, north, res, src, scaled, pot, down, up, above, below,
+    shifts, helm, raw, coded, x, frac, field, adv, north, res, src, scaled, pot, down, up, above, below,
     small, in_send, in_recv, halo_send, halo_recv, out_send, out_recv,
 ):
     n_cols = n_lon * fields.shape[3]
@@ -70,13 +70,6 @@
     def wrap(k):
         return k & (n_chunks - 1)
 
-    def each_group(turn):
-        def body(g, _):
-            turn(g * GROUP)
-            return 0
-
-        lax.fori_loop(0, n_chunks // GROUP, body, 0)
-
     barrier = pltpu.get_barrier_semaphore()
 
     def greet(j, _):
@@ -90,13 +83,18 @@
 
     get_shifts = pltpu.make_async_copy(shifts_hbm, shifts, small.at[0])
     get_helm = pltpu.make_async_copy(helm_hbm, helm, small.at[1])
+    get_fractions = [
+        pltpu.make_async_copy(fractions.at[step], raw.at[step], small.at[2 + step]) for step in range(STEPS)
+    ]
+    for c in get_fractions:
+        c.start()
     get_shifts.start()
     get_helm.start()
 
     zero = jnp.zeros((8, LANES), F32)
 
     def clear(base):
-        for j in range(GROUP):
+        for j in range(n_chunks):
             k = base + j
             north[k, 0:8] = zero
             north[k, 24:32] = zero
@@ -104,52 +102,59 @@
                 pot[i, k, 0:8] = zero
                 pot[i, k, 40:48] = zero
 
-    each_group(clear)
+    clear(0)
     pl.semaphore_wait(barrier, n_lon + 1)
 
     def in_refs(part, to_block, to_level, from_lon):
-        if part == 0:
-            return (fields.at[0:3, to_level, rows_of(to_block), :], x.at[0:3, :, cols_of(from_lon)])
-        if part == 2:
-            return (fields.at[3, to_level, rows_of(to_block), :], x.at[3, :, cols_of(from_lon)])
-        step = part // 2
-        return (fractions.at[step, rows_of(to_block), :], frac.at[step, :, cols_of(from_lon)])
-
-    def send_parts(parts):
+        if part < 4:
+            return (fields.at[part, to_level, rows_of(to_block), :], x.at[part, :, cols_of(from_lon)])
+        return (coded.at[part - 4, rows_of(to_block), :], frac.at[part - 4, :, cols_of(from_lon)])
+
+    def send_part(part):
         def turn(j, _):
             peer = lax.rem(lon + j, n_lon)
             to_block, to_level = place_of(peer)
-            for part in parts:
-                from_ref, to_ref = in_refs(part, to_block, to_level, lon)
-                pltpu.make_async_remote_copy(
-                    src_ref=from_ref,
-                    dst_ref=to_ref,
-                    send_sem=in_send.at[part],
-                    recv_sem=in_recv.at[part],
-                    device_id={"lon": peer, "lat": lat},
-                    device_id_type=MESH,
-                ).start()
+            from_ref, to_ref = in_refs(part, to_block, to_level, lon)
+            pltpu.make_async_remote_copy(
+                src_ref=from_ref,
+                dst_ref=to_ref,
+                send_sem=in_send.at[part],
+                recv_sem=in_recv.at[part],
+                device_id={"lon": peer, "lat": lat},
+                device_id_type=MESH,
+            ).start()
             return 0
 
         lax.fori_loop(1, n_lon, turn, 0)
-        for part in parts:
-            from_ref, to_ref = in_refs(part, block, level, lon)
-            pltpu.make_async_copy(from_ref, to_ref, in_recv.at[part]).start()
+        from_ref, to_ref = in_refs(part, block, level, lon)
+        pltpu.make_async_copy(from_ref, to_ref, in_recv.at[part]).start()
 
     def in_whole(part):
-        return (x.at[0:3], frac.at[0], x.at[3], frac.at[1])[part]
+        return x.at[part] if part < 4 else frac.at[part - 4]
 
     def wait_in(part):
         whole = in_whole(part)
         pltpu.make_async_copy(whole, whole, in_recv.at[part]).wait()
 
     def wait_in_sent(part):
-        whole = in_whole(part)
-        sent = whole.at[:, :, 0 : n_cols - tile] if part == 0 else whole.at[:, 0 : n_cols - tile]
+        sent = in_whole(part).at[:, 0 : n_cols - tile]
         pltpu.make_async_copy(sent, sent, in_send.at[part]).wait()
 
-    send_parts((0, 1))
-    send_parts((2, 3))
+    def code(step):
+        get_fractions[step].wait()
+        coded[step] = ((raw[step] * UNITS + 0.5).astype(jnp.int32) - HALF).astype(jnp.int16)
+
+    def decode(value):
+        return value.astype(jnp.int32).astype(F32) * (1.0 / UNITS) + HALF / UNITS
+
+    send_part(0)
+    code(0)
+    send_part(4)
+    send_part(1)
+    send_part(2)
+    code(1)
+    send_part(3)
+    send_part(5)
     get_shifts.wait()
     get_helm.wait()
 
@@ -165,11 +170,11 @@
 
     def unpack(parts):
         def turn(base):
-            for j in range(GROUP):
+            for j in range(n_chunks):
                 for f in parts:
                     field[f, base + j] = x[f, :, chunk(base + j)].astype(F32)
 
-        each_group(turn)
+        turn(0)
 
     def advect(step, sources, targets):
         shift = shifts[step, block]
@@ -180,38 +185,43 @@
         from_here = [lane16 >= part for _, part in taps]
 
         def turn(base):
-            weights = [cubic_weights(frac[step, :, chunk(base + j)]) for j in range(GROUP)]
+            weights = [cubic_weights(decode(frac[step, :, chunk(base + j)])) for j in range(n_chunks)]
             for f, to in zip(sources, targets):
-                total = [None] * GROUP
+                total = [None] * n_chunks
                 for tap, (whole, part) in enumerate(taps):
                     before = None
-                    for j in range(-1, GROUP):
+                    for j in range(-1, n_chunks):
                         here = pltpu.roll(field[f, wrap(base + j - whole + n_chunks)], part, 1)
                         if j >= 0:
                             term = weights[j][tap] * jnp.where(from_here[tap], here, before)
                             total[j] = term if tap == 0 else total[j] + term
                         before = here
-                for j in range(GROUP):
+                for j in range(n_chunks):
                     to(base + j, total[j].astype(BF16))
 
-        each_group(turn)
+        turn(0)
 
     def east_west(base, count, load):
-        vals = [load(wrap(base - 1 + n_chunks))] + [load(base + j) for j in range(count)]
-        vals.append(load(wrap(base + count)))
-        ln = lax.broadcasted_iota(jnp.int32, vals[0].shape, 1)
+        mid = load(base)
+        ln = lax.broadcasted_iota(jnp.int32, mid.shape, 1)
         last, first = ln == LANES - 1, ln == 0
-        east = [None] + [pltpu.roll(v, LANES - 1, 1) for v in vals[1:]]
-        west = [pltpu.roll(v, 1, 1) for v in vals[:-1]]
-        return [
-            (vals[j], jnp.where(last, east[j + 1], east[j]), jnp.where(first, west[j - 1], west[j]))
-            for j in range(1, count + 1)
-        ]
+        before = pltpu.roll(load(wrap(base - 1 + n_chunks)), 1, 1)
+        mid_east = pltpu.roll(mid, LANES - 1, 1)
+        for j in range(count):
+            after = load(wrap(base + j + 1))
+            after_east = pltpu.roll(after, LANES - 1, 1)
+            mid_west = pltpu.roll(mid, 1, 1)
+            yield (
+                base + j,
+                mid,
+                jnp.where(last, after_east, mid_east),
+                jnp.where(first, before, mid_west),
+            )
+            mid, mid_east, before = after, after_east, mid_west
 
     def sources(step):
         def turn(base):
-            for j, (_, e, w) in enumerate(east_west(base, GROUP, lambda k: adv[1, k])):
-                k = base + j
+            for k, _, e, w in east_west(base, n_chunks, lambda k: adv[1, k]):
                 own = adv[0, k] - 0.25 * ((e - w) + (north[k, 9:25] - north[k, 7:23]))
                 src[k, ROWS : 2 * ROWS] = own
                 top, bottom = own[0:8], own[8:16]
@@ -220,7 +230,7 @@
                 down[step, k] = jnp.concatenate([with_last, bottom], axis=0).astype(BF16)
                 up[step, k] = jnp.concatenate([top, with_first], axis=0).astype(BF16)
 
-        each_group(turn)
+        turn(0)
 
     def halo_copies(step):
         return (
@@ -246,7 +256,7 @@
         first_has, last_has = (row8 == 0) & has_below, (row8 == 7) & has_above
 
         def turn(base):
-            for j in range(GROUP):
+            for j in range(n_chunks):
                 k = base + j
                 a = jnp.where(has_above, above[step, k].astype(F32), 0.0)
                 b = jnp.where(has_below, below[step, k].astype(F32), 0.0)
@@ -257,47 +267,44 @@
                 src[k, 32:40] = b[0:8] + jnp.where(first_has, 0.25 * north[k, 23:31], 0.0)
                 src[k, 40:48] = b[8:16]
 
-        each_group(turn)
+        turn(0)
 
     def first_sweep():
         weight, inverse = weight_of(8, 2 * ROWS)
 
         def turn(base):
-            for j, (mid, e, w) in enumerate(east_west(base, GROUP, lambda k: src[k, 8:40])):
-                k = base + j
+            for k, mid, e, w in east_west(base, n_chunks, lambda k: src[k, 8:40]):
                 fixed = mid * inverse
                 scaled[k] = fixed
                 pot[0, k, 8:40] = fixed + weight * ((e + w) + (src[k, 7:39] + src[k, 9:41]))
 
-        each_group(turn)
-
-    def later_sweeps(begin, end, start, rows):
-        weight, _ = weight_of(start, rows)
-
-        def sweep(i, _):
-            now, then = i & 1, (i + 1) & 1
-
-            def turn(base):
-                for j, (_, e, w) in enumerate(
-                    east_west(base, GROUP, lambda k: pot[now, k, start : start + rows])
-                ):
-                    k = base + j
-                    n = pot[now, k, start - 1 : start - 1 + rows]
-                    s = pot[now, k, start + 1 : start + 1 + rows]
-                    fixed = scaled[k, start - 8 : start - 8 + rows]
-                    pot[then, k, start : start + rows] = fixed + weight * ((e + w) + (n + s))
-
-            each_group(turn)
+        turn(0)
+
+    def later_sweeps():
+        def sweep(now, start, weight):
+            rows = weight.shape[0]
+            for k, _, e, w in east_west(0, n_chunks, lambda k: pot[now, k, start : start + rows]):
+                n = pot[now, k, start - 1 : start - 1 + rows]
+                s = pot[now, k, start + 1 : start + 1 + rows]
+                fixed = scaled[k, start - 8 : start - 8 + rows]
+                pot[1 - now, k, start : start + rows] = fixed + weight * ((e + w) + (n + s))
+
+        wide, _ = weight_of(8, 32)
+        narrow, _ = weight_of(12, 24)
+
+        def pair(i, _):
+            sweep(0, 8, wide)
+            sweep(1, 8, wide)
             return 0
 
-        lax.fori_loop(begin, end, sweep, 0)
+        lax.fori_loop(0, 2, pair, 0)
+        for i in range(4, SWEEPS - 1):
+            sweep(i % 2, 12, narrow)
 
     solved = (SWEEPS - 1) % 2
 
     def update(base, count, to):
-        own = east_west(base, count, lambda k: pot[solved, k, ROWS : 2 * ROWS])
-        for j, (mid, e, w) in enumerate(own):
-            k = base + j
+        for k, mid, e, w in east_west(base, count, lambda k: pot[solved, k, ROWS : 2 * ROWS]):
             n, s = pot[solved, k, ROWS - 1 : 2 * ROWS - 1], pot[solved, k, ROWS + 1 : 2 * ROWS + 1]
             to(0, k, mid.astype(BF16))
             to(1, k, (adv[1, k] - 0.25 * (e - w)).astype(BF16))
@@ -351,18 +358,20 @@
     for step in range(STEPS):
         last = step == STEPS - 1
         if step == 0:
-            wait_in(0)
-            wait_in(1)
-            unpack((0, 1, 2))
+            wait_in(4)
+            for f in range(3):
+                wait_in(f)
+                unpack((f,))
+                advect(step, [f], [functools.partial(to_adv, f)])
         else:
-            wait_in(3)
-        advect(step, range(3), [functools.partial(to_adv, f) for f in range(3)])
+            wait_in(5)
+            advect(step, range(3), [functools.partial(to_adv, f) for f in range(3)])
         sources(step)
         copies = halo_copies(step)
         for c in copies:
             c.start()
         if step == 0:
-            wait_in(2)
+            wait_in(3)
             unpack((3,))
         advect(step, [3 + step], [functools.partial(to_res if last else to_field, 3 + (not last))])
         if last:
@@ -377,14 +386,13 @@
             c.wait_recv()
         complete(step)
         first_sweep()
-        later_sweeps(0, 3, 8, 32)
-        later_sweeps(3, SWEEPS - 1, 12, 24)
+        later_sweeps()
         if last:
             update_and_send()
         else:
-            each_group(lambda base: update(base, GROUP, to_field))
-
-    for part in range(4):
+            update(0, n_chunks, to_field)
+
+    for part in range(6):
         wait_in_sent(part)
     for step in range(STEPS):
         for c in halo_copies(step):
@@ -407,8 +415,10 @@
         scratch_shapes=[
             pltpu.SMEM(shifts.shape, jnp.int32),
             pltpu.SMEM(helm_coef.shape, F32),
+            pltpu.VMEM(fractions.shape, F32),
+            pltpu.VMEM(fractions.shape, jnp.int16),
             pltpu.VMEM((4, ROWS, n_cols), BF16),
-            pltpu.VMEM((STEPS, ROWS, n_cols), F32),
+            pltpu.VMEM((STEPS, ROWS, n_cols), jnp.int16),
             pltpu.VMEM((5, n_chunks, ROWS, LANES), F32),
             pltpu.VMEM((2, n_chunks, ROWS, LANES), F32),
             pltpu.VMEM((n_chunks, 2 * ROWS, LANES), F32),
@@ -420,9 +430,9 @@
             pltpu.VMEM((STEPS, n_chunks, ROWS, LANES), BF16),
             pltpu.VMEM((STEPS, n_chunks, ROWS, LANES), BF16),
             pltpu.VMEM((STEPS, n_chunks, ROWS, LANES), BF16),
-            pltpu.SemaphoreType.DMA((2,)),
-            pltpu.SemaphoreType.DMA((4,)),
-            pltpu.SemaphoreType.DMA((4,)),
+            pltpu.SemaphoreType.DMA((2 + STEPS,)),
+            pltpu.SemaphoreType.DMA((4 + STEPS,)),
+            pltpu.SemaphoreType.DMA((4 + STEPS,)),
             pltpu.SemaphoreType.DMA((STEPS, 2)),
             pltpu.SemaphoreType.DMA((STEPS, 2)),
             pltpu.SemaphoreType.DMA((2,)),

time: 46.7 us -> 42.5 us (0.910)
  Pallas kernels: 45.8 us -> 41.6 us
    pallas_call x1, Pallas kernels: 45.8 us -> 41.6 us  [local(): pl.pallas_call(functools.partial(kernel, n_lon, n_lat), out_shape=jax.Sha...]
where the time goes in v3:
time: 42.5 us; the launch traced here: 42.4 us
  Pallas kernels  41.6 us (98%)
  local copies, waits for them, and re-layouts  0.8 us (2%)
    pallas_call x1, Pallas kernels, local(): pl.pallas_call(functools.partial(kernel, n_lon, n_lat), out_shape=jax.Sha...  41.6 us

profile of v3, /device:TPU:1, one launch (start us, length us, event | category | flops | bytes accessed | tf_op | source)
XLA Modules:
  0.0 42.4 jit_solution(13894485064556615884)
XLA Ops:
  0.0 41.6 %transport.1 = bf16[4,2,128,256]{3,2,1,0:T(8,128)(2,1)S(1)} custom-call(bf16[4,2,128,256]{3,2,1,0:T(8,128)(2,1)} %fields.1, s32[2,8]{1,0:T(2,128)} %shifts_hbm.1, f32[2,128,256]{2,1,0:T(8,128)} %fractions.1, f32[2]{0:T(128)} %helm_hbm.1), custom_call_target="tpu_custom_call" | custom-call | tf_op jit(solution)/shard_map/transport/pallas_call | solution.py:410
  41.6 0.8 %copy.6 = bf16[4,2,128,256]{3,2,1,0:T(8,128)(2,1)} copy(bf16[4,2,128,256]{3,2,1,0:T(8,128)(2,1)S(1)} %transport.1) | data formatting | bytes 1048576

commit v4 on v3

--- a/solution.py
+++ b/solution.py
@@ -17,12 +17,16 @@
 MESH = pl.DeviceIdType.MESH
 
 
-def place_of(lon):
-    return 2 * (lon // 4) + lon % 2, (lon // 2) % 2
-
-
-def lon_of(block, level):
-    return 4 * (block // 2) + 2 * level + block % 2
+def place_of(lon, lat, n_blocks):
+    along = 2 * lax.div(lon, 4) + lax.rem(lon, 2)
+    odd = lax.rem(lat, 2)
+    return along + odd * (n_blocks - 1 - 2 * along), lax.rem(lax.div(lon, 2), 2)
+
+
+def lon_of(block, level, lat, n_blocks):
+    odd = lax.rem(lat, 2)
+    along = block + odd * (n_blocks - 1 - 2 * block)
+    return 4 * lax.div(along, 2) + 2 * level + lax.rem(along, 2)
 
 
 def cubic_weights(a):
@@ -46,14 +50,14 @@
     n_chunks = n_cols // LANES
     n_blocks = fields.shape[2] // ROWS
     lon, lat = lax.axis_index("lon"), lax.axis_index("lat")
-    block, level = place_of(lon)
+    block, level = place_of(lon, lat, n_blocks)
 
     prev_block = lax.rem(block + n_blocks - 1, n_blocks)
     next_block = lax.rem(block + 1, n_blocks)
     lat_up = lax.rem(lat + n_lat - (block == 0).astype(jnp.int32), n_lat)
     lat_down = lax.rem(lat + (block == n_blocks - 1).astype(jnp.int32), n_lat)
-    dev_up = {"lon": lon_of(prev_block, level), "lat": lat_up}
-    dev_down = {"lon": lon_of(next_block, level), "lat": lat_down}
+    dev_up = {"lon": lon_of(prev_block, level, lat_up, n_blocks), "lat": lat_up}
+    dev_down = {"lon": lon_of(next_block, level, lat_down, n_blocks), "lat": lat_down}
     row_block = lat * n_blocks + block
     has_above = row_block > 0
     has_below = row_block < n_lat * n_blocks - 1
@@ -113,7 +117,7 @@
     def send_part(part):
         def turn(j, _):
             peer = lax.rem(lon + j, n_lon)
-            to_block, to_level = place_of(peer)
+            to_block, to_level = place_of(peer, lat, n_blocks)
             from_ref, to_ref = in_refs(part, to_block, to_level, lon)
             pltpu.make_async_remote_copy(
                 src_ref=from_ref,

time: 42.5 us -> 41.5 us (0.976)
  Pallas kernels: 41.6 us -> 40.6 us
    pallas_call x1, Pallas kernels: 41.6 us -> 40.6 us  [local(): pl.pallas_call(functools.partial(kernel, n_lon, n_lat), out_shape=jax.Sha...]
where the time goes in v4:
time: 41.5 us; the launch traced here: 41.4 us
  Pallas kernels  40.6 us (98%)
  local copies, waits for them, and re-layouts  0.8 us (2%)
    pallas_call x1, Pallas kernels, local(): pl.pallas_call(functools.partial(kernel, n_lon, n_lat), out_shape=jax.Sha...  40.6 us

profile of v4, /device:TPU:1, one launch (start us, length us, event | category | flops | bytes accessed | tf_op | source)
XLA Modules:
  0.0 41.4 jit_solution(6864515281226694925)
XLA Ops:
  0.0 40.6 %transport.1 = bf16[4,2,128,256]{3,2,1,0:T(8,128)(2,1)S(1)} custom-call(bf16[4,2,128,256]{3,2,1,0:T(8,128)(2,1)} %fields.1, s32[2,8]{1,0:T(2,128)} %shifts_hbm.1, f32[2,128,256]{2,1,0:T(8,128)} %fractions.1, f32[2]{0:T(128)} %helm_hbm.1), custom_call_target="tpu_custom_call" | custom-call | tf_op jit(solution)/shard_map/transport/pallas_call | solution.py:414
  40.6 0.8 %copy.6 = bf16[4,2,128,256]{3,2,1,0:T(8,128)(2,1)} copy(bf16[4,2,128,256]{3,2,1,0:T(8,128)(2,1)S(1)} %transport.1) | data formatting | bytes 1048576

commit v5 on v4

--- a/solution.py
+++ b/solution.py
@@ -11,6 +11,8 @@
 SWEEPS = 8
 ROWS = 16
 LANES = 128
+WAYS = 4
+WINDOW = WAYS * LANES
 F32 = jnp.float32
 BF16 = jnp.bfloat16
 UNITS, HALF = 65535.0, 32768
@@ -42,12 +44,13 @@
 
 def kernel(
     n_lon, n_lat, fields, shifts_hbm, fractions, helm_hbm, out,
-    shifts, helm, raw, coded, x, frac, field, adv, north, res, src, scaled, pot, down, up, above, below,
+    shifts, helm, raw, coded, deal, gather, x, frac, share, field, adv, north, res, src, scaled, pot, down, up, above, below,
     small, in_send, in_recv, halo_send, halo_recv, out_send, out_recv,
 ):
     n_cols = n_lon * fields.shape[3]
     tile = fields.shape[3]
     n_chunks = n_cols // LANES
+    n_windows = n_cols // WINDOW
     n_blocks = fields.shape[2] // ROWS
     lon, lat = lax.axis_index("lon"), lax.axis_index("lat")
     block, level = place_of(lon, lat, n_blocks)
@@ -68,11 +71,11 @@
     def cols_of(p):
         return pl.ds(pl.multiple_of(p * tile, tile), tile)
 
-    def chunk(k):
-        return pl.ds(pl.multiple_of(k * LANES, LANES), LANES)
-
-    def wrap(k):
-        return k & (n_chunks - 1)
+    def window(w):
+        return pl.ds(pl.multiple_of(w * WINDOW, WINDOW), WINDOW)
+
+    def wrap(w):
+        return w & (n_windows - 1)
 
     barrier = pltpu.get_barrier_semaphore()
 
@@ -94,6 +97,11 @@
         c.start()
     get_shifts.start()
     get_helm.start()
+
+    row = lax.broadcasted_iota(jnp.int32, (WINDOW, WINDOW), 0)
+    col = lax.broadcasted_iota(jnp.int32, (WINDOW, WINDOW), 1)
+    deal[...] = jnp.where(row == WAYS * ((col & (LANES - 1))) + (col >> 7), 1.0, 0.0).astype(BF16)
+    gather[...] = jnp.where(col == WAYS * ((row & (LANES - 1))) + (row >> 7), 1.0, 0.0).astype(BF16)
 
     zero = jnp.zeros((8, LANES), F32)
 
@@ -148,9 +156,6 @@
         get_fractions[step].wait()
         coded[step] = ((raw[step] * UNITS + 0.5).astype(jnp.int32) - HALF).astype(jnp.int16)
 
-    def decode(value):
-        return value.astype(jnp.int32).astype(F32) * (1.0 / UNITS) + HALF / UNITS
-
     send_part(0)
     code(0)
     send_part(4)
@@ -172,60 +177,76 @@
         inside = ((row >= ROWS) | has_above) & ((row < 2 * ROWS) | has_below)
         return jnp.where(inside, coef * inverse, 0.0), inverse
 
-    def unpack(parts):
-        def turn(base):
-            for j in range(n_chunks):
-                for f in parts:
-                    field[f, base + j] = x[f, :, chunk(base + j)].astype(F32)
-
-        turn(0)
+    def dealt(rows):
+        return jnp.dot(jnp.concatenate(rows, axis=0), deal[...], preferred_element_type=F32)
+
+    def natural(rows):
+        return jnp.dot(jnp.concatenate(rows, axis=0), gather[...], preferred_element_type=F32)
+
+    def piece(values, i, m):
+        return values[i * ROWS : (i + 1) * ROWS, m * LANES : (m + 1) * LANES]
+
+    def unpack(f):
+        values = dealt([x[f, :, window(w)] for w in range(n_windows)])
+        for w in range(n_windows):
+            for m in range(WAYS):
+                field[f, WAYS * w + m] = piece(values, w, m)
+
+    def unpack_fractions(step):
+        rows = [frac[step, :, window(w)].astype(jnp.int32) + HALF for w in range(n_windows)]
+        high = dealt([(r >> 8).astype(F32).astype(BF16) for r in rows])
+        low = dealt([(r & 255).astype(F32).astype(BF16) for r in rows])
+        values = (high * 256.0 + low) * (1.0 / UNITS)
+        for w in range(n_windows):
+            for m in range(WAYS):
+                share[step, WAYS * w + m] = piece(values, w, m)
 
     def advect(step, sources, targets):
         shift = shifts[step, block]
         taps = []
-        for d in (1, 0, -1, -2):
-            total = (shift + (n_cols - d)) & (n_cols - 1)
-            taps.append((total // LANES, total & (LANES - 1)))
-        from_here = [lane16 >= part for _, part in taps]
-
-        def turn(base):
-            weights = [cubic_weights(decode(frac[step, :, chunk(base + j)])) for j in range(n_chunks)]
-            for f, to in zip(sources, targets):
-                total = [None] * n_chunks
-                for tap, (whole, part) in enumerate(taps):
-                    before = None
-                    for j in range(-1, n_chunks):
-                        here = pltpu.roll(field[f, wrap(base + j - whole + n_chunks)], part, 1)
-                        if j >= 0:
-                            term = weights[j][tap] * jnp.where(from_here[tap], here, before)
-                            total[j] = term if tap == 0 else total[j] + term
-                        before = here
-                for j in range(n_chunks):
-                    to(base + j, total[j].astype(BF16))
-
-        turn(0)
+        for t in range(-2, WAYS + 1):
+            back = (shift + (n_cols - t)) & (n_cols - 1)
+            way = (n_cols - back) & (WAYS - 1)
+            cells = (back + way) // WAYS
+            taps.append((way, cells // LANES, cells & (LANES - 1)))
+        from_here = [lane16 >= part for _, _, part in taps]
+
+        def rolled(f, w, tap):
+            way, whole, part = taps[tap]
+            return pltpu.roll(field[f, WAYS * wrap(w - whole + 2 * n_windows) + way], part, 1)
+
+        for f, to in zip(sources, targets):
+            before = [rolled(f, -1, tap) for tap in range(len(taps))]
+            for w in range(n_windows):
+                here = [rolled(f, w, tap) for tap in range(len(taps))]
+                values = [jnp.where(c, h, b) for c, h, b in zip(from_here, here, before)]
+                before = here
+                for m in range(WAYS):
+                    k = WAYS * w + m
+                    w0, w1, w2, w3 = cubic_weights(share[step, k])
+                    total = w0 * values[m + 3] + w1 * values[m + 2] + w2 * values[m + 1] + w3 * values[m]
+                    to(k, total.astype(BF16))
 
     def east_west(base, count, load):
-        mid = load(base)
-        ln = lax.broadcasted_iota(jnp.int32, mid.shape, 1)
+        before = pltpu.roll(load(WAYS * wrap(base - 1 + n_windows) + WAYS - 1), 1, 1)
+        start = load(WAYS * base)
+        start_east = pltpu.roll(start, LANES - 1, 1)
+        ln = lax.broadcasted_iota(jnp.int32, start.shape, 1)
         last, first = ln == LANES - 1, ln == 0
-        before = pltpu.roll(load(wrap(base - 1 + n_chunks)), 1, 1)
-        mid_east = pltpu.roll(mid, LANES - 1, 1)
         for j in range(count):
-            after = load(wrap(base + j + 1))
+            vals = [start] + [load(WAYS * (base + j) + m) for m in range(1, WAYS)]
+            after = load(WAYS * wrap(base + j + 1))
             after_east = pltpu.roll(after, LANES - 1, 1)
-            mid_west = pltpu.roll(mid, 1, 1)
-            yield (
-                base + j,
-                mid,
-                jnp.where(last, after_east, mid_east),
-                jnp.where(first, before, mid_west),
-            )
-            mid, mid_east, before = after, after_east, mid_west
+            end_west = pltpu.roll(vals[-1], 1, 1)
+            east = vals[1:] + [jnp.where(last, after_east, start_east)]
+            west = [jnp.where(first, before, end_west)] + vals[:-1]
+            for m in range(WAYS):
+                yield WAYS * (base + j) + m, vals[m], east[m], west[m]
+            start, start_east, before = after, after_east, end_west
 
     def sources(step):
         def turn(base):
-            for k, _, e, w in east_west(base, n_chunks, lambda k: adv[1, k]):
+            for k, _, e, w in east_west(base, n_windows, lambda k: adv[1, k]):
                 own = adv[0, k] - 0.25 * ((e - w) + (north[k, 9:25] - north[k, 7:23]))
                 src[k, ROWS : 2 * ROWS] = own
                 top, bottom = own[0:8], own[8:16]
@@ -277,7 +298,7 @@
         weight, inverse = weight_of(8, 2 * ROWS)
 
         def turn(base):
-            for k, mid, e, w in east_west(base, n_chunks, lambda k: src[k, 8:40]):
+            for k, mid, e, w in east_west(base, n_windows, lambda k: src[k, 8:40]):
                 fixed = mid * inverse
                 scaled[k] = fixed
                 pot[0, k, 8:40] = fixed + weight * ((e + w) + (src[k, 7:39] + src[k, 9:41]))
@@ -287,7 +308,7 @@
     def later_sweeps():
         def sweep(now, start, weight):
             rows = weight.shape[0]
-            for k, _, e, w in east_west(0, n_chunks, lambda k: pot[now, k, start : start + rows]):
+            for k, _, e, w in east_west(0, n_windows, lambda k: pot[now, k, start : start + rows]):
                 n = pot[now, k, start - 1 : start - 1 + rows]
                 s = pot[now, k, start + 1 : start + 1 + rows]
                 fixed = scaled[k, start - 8 : start - 8 + rows]
@@ -316,9 +337,6 @@
 
     def to_field(f, k, value):
         field[f, k] = value.astype(F32)
-
-    def to_res(f, k, value):
-        res[f, :, chunk(k)] = value
 
     def to_adv(f, k, value):
         if f == 2:
@@ -344,31 +362,44 @@
         )
 
     def update_and_send():
-        per = tile // LANES
+        per = WINDOW // tile
+        core = lax.rem(lon, 2)
 
         def turn(j, _):
-            peer = lax.rem(lon + j, n_lon)
-            update(peer * per, per, to_res)
-
-            @pl.when(j < n_lon)
-            def _():
-                out_copy(0, peer).start()
+            w = wrap(lax.div(lon, per) + j + core * (n_windows - 2 * j))
+            made = {}
+            update(w, 1, lambda f, k, value: made.setdefault(f, []).append(value))
+            rows = natural([jnp.concatenate(made[f], axis=1) for f in range(3)])
+            for f in range(3):
+                res[f, :, window(w)] = rows[f * ROWS : (f + 1) * ROWS].astype(BF16)
+            for i in range(per):
+                peer = per * w + i
+
+                @pl.when(peer != lon)
+                def _():
+                    out_copy(0, peer).start()
 
             return 0
 
-        lax.fori_loop(1, n_lon + 1, turn, 0)
+        lax.fori_loop(1, n_windows + 1, turn, 0)
         out_keep(0).start()
+
+    def restore(f):
+        chunks = [field[f, k].astype(BF16) for k in range(n_chunks)]
+        rows = natural([jnp.concatenate(chunks[WAYS * w : WAYS * (w + 1)], axis=1) for w in range(n_windows)])
+        for w in range(n_windows):
+            res[f, :, window(w)] = rows[w * ROWS : (w + 1) * ROWS].astype(BF16)
 
     for step in range(STEPS):
         last = step == STEPS - 1
         if step == 0:
             wait_in(4)
+            unpack_fractions(0)
             for f in range(3):
                 wait_in(f)
-                unpack((f,))
+                unpack(f)
                 advect(step, [f], [functools.partial(to_adv, f)])
         else:
-            wait_in(5)
             advect(step, range(3), [functools.partial(to_adv, f) for f in range(3)])
         sources(step)
         copies = halo_copies(step)
@@ -376,9 +407,12 @@
             c.start()
         if step == 0:
             wait_in(3)
-            unpack((3,))
-        advect(step, [3 + step], [functools.partial(to_res if last else to_field, 3 + (not last))])
+            unpack(3)
+            wait_in(5)
+            unpack_fractions(1)
+        advect(step, [3 + step], [functools.partial(to_field, 4 - step)])
         if last:
+            restore(3)
 
             def send_res3(j, _):
                 out_copy(1, lax.rem(lon + j, n_lon)).start()
@@ -394,7 +428,7 @@
         if last:
             update_and_send()
         else:
-            update(0, n_chunks, to_field)
+            update(0, n_windows, to_field)
 
     for part in range(6):
         wait_in_sent(part)
@@ -421,8 +455,11 @@
             pltpu.SMEM(helm_coef.shape, F32),
             pltpu.VMEM(fractions.shape, F32),
             pltpu.VMEM(fractions.shape, jnp.int16),
+            pltpu.VMEM((WINDOW, WINDOW), BF16),
+            pltpu.VMEM((WINDOW, WINDOW), BF16),
             pltpu.VMEM((4, ROWS, n_cols), BF16),
             pltpu.VMEM((STEPS, ROWS, n_cols), jnp.int16),
+            pltpu.VMEM((STEPS, n_chunks, ROWS, LANES), F32),
             pltpu.VMEM((5, n_chunks, ROWS, LANES), F32),
             pltpu.VMEM((2, n_chunks, ROWS, LANES), F32),
             pltpu.VMEM((n_chunks, 2 * ROWS, LANES), F32),

time: 41.5 us -> 38.4 us (0.925)
  Pallas kernels: 40.6 us -> 37.5 us
    pallas_call x1, Pallas kernels: 40.6 us -> 37.5 us  [local(): pl.pallas_call(functools.partial(kernel, n_lon, n_lat), out_shape=jax.Sha...]
where the time goes in v5:
time: 38.4 us; the launch traced here: 38.3 us
  Pallas kernels  37.5 us (98%)
  local copies, waits for them, and re-layouts  0.8 us (2%)
    pallas_call x1, Pallas kernels, local(): pl.pallas_call(functools.partial(kernel, n_lon, n_lat), out_shape=jax.Sha...  37.5 us
    unnamed x1, local copies, waits for them, and re-layouts  0.8 us

profile of v5, /device:TPU:1, one launch (start us, length us, event | category | flops | bytes accessed | tf_op | source)
XLA Modules:
  0.0 38.3 jit_solution(15105624077516662934)
XLA Ops:
  0.0 37.5 %transport.1 = bf16[4,2,128,256]{3,2,1,0:T(8,128)(2,1)S(1)} custom-call(bf16[4,2,128,256]{3,2,1,0:T(8,128)(2,1)} %fields.1, s32[2,8]{1,0:T(2,128)} %shifts_hbm.1, f32[2,128,256]{2,1,0:T(8,128)} %fractions.1, f32[2]{0:T(128)} %helm_hbm.1), custom_call_target="tpu_custom_call" | custom-call | tf_op jit(solution)/shard_map/transport/pallas_call | solution.py:448
  37.5 0.8 %copy.6 = bf16[4,2,128,256]{3,2,1,0:T(8,128)(2,1)} copy(bf16[4,2,128,256]{3,2,1,0:T(8,128)(2,1)S(1)} %transport.1) | data formatting | bytes 1048576

commit v6 on v5

--- a/solution.py
+++ b/solution.py
@@ -44,7 +44,7 @@
 
 def kernel(
     n_lon, n_lat, fields, shifts_hbm, fractions, helm_hbm, out,
-    shifts, helm, raw, coded, deal, gather, x, frac, share, field, adv, north, res, src, scaled, pot, down, up, above, below,
+    shifts, helm, raw, coded, deal, gather, x, frac, share, field, adv, north, res, src, edge, scaled, pot, down, up, above, below,
     small, in_send, in_recv, halo_send, halo_recv, out_send, out_recv,
 ):
     n_cols = n_lon * fields.shape[3]
@@ -249,13 +249,17 @@
             for k, _, e, w in east_west(base, n_windows, lambda k: adv[1, k]):
                 own = adv[0, k] - 0.25 * ((e - w) + (north[k, 9:25] - north[k, 7:23]))
                 src[k, ROWS : 2 * ROWS] = own
-                top, bottom = own[0:8], own[8:16]
-                with_last = jnp.where(row8 == 0, north[k, 23:31], top)
-                with_first = jnp.where(row8 == 7, north[k, 1:9], bottom)
-                down[step, k] = jnp.concatenate([with_last, bottom], axis=0).astype(BF16)
-                up[step, k] = jnp.concatenate([top, with_first], axis=0).astype(BF16)
+                down[step, k] = own[8:16].astype(BF16)
+                up[step, k] = own[0:8].astype(BF16)
+                edge[0, k : k + 1] = src[k, 23:24]
+                edge[0, n_chunks + k : n_chunks + k + 1] = north[k, 23:24]
+                edge[1, k : k + 1] = src[k, 24:25]
+                edge[1, n_chunks + k : n_chunks + k + 1] = north[k, 8:9]
 
         turn(0)
+        for i in range(n_chunks // 4):
+            down[step, n_chunks + i] = edge[0, 8 * i : 8 * i + 8].astype(BF16)
+            up[step, n_chunks + i] = edge[1, 8 * i : 8 * i + 8].astype(BF16)
 
     def halo_copies(step):
         return (
@@ -279,20 +283,20 @@
 
     def complete(step):
         first_has, last_has = (row8 == 0) & has_below, (row8 == 7) & has_above
-
-        def turn(base):
-            for j in range(n_chunks):
-                k = base + j
-                a = jnp.where(has_above, above[step, k].astype(F32), 0.0)
-                b = jnp.where(has_below, below[step, k].astype(F32), 0.0)
-                src[k, 0:8] = a[0:8]
-                src[k, 8:16] = a[8:16] - jnp.where(last_has, 0.25 * north[k, 1:9], 0.0)
-                src[k, 16:24] = src[k, 16:24] + jnp.where(row8 == 0, 0.25 * a[0:8], 0.0)
-                src[k, 24:32] = src[k, 24:32] - jnp.where(row8 == 7, 0.25 * b[8:16], 0.0)
-                src[k, 32:40] = b[0:8] + jnp.where(first_has, 0.25 * north[k, 23:31], 0.0)
-                src[k, 40:48] = b[8:16]
-
-        turn(0)
+        for i in range(n_chunks // 4):
+            a = above[step, n_chunks + i].astype(F32)
+            b = below[step, n_chunks + i].astype(F32)
+            edge[0, 8 * i : 8 * i + 8] = jnp.where(has_above, a, 0.0)
+            edge[1, 8 * i : 8 * i + 8] = jnp.where(has_below, b, 0.0)
+        for k in range(n_chunks):
+            a = jnp.where(has_above, above[step, k].astype(F32), 0.0)
+            b = jnp.where(has_below, below[step, k].astype(F32), 0.0)
+            src[k, 8:16] = a - jnp.where(last_has, 0.25 * north[k, 1:9], 0.0)
+            src[k, 32:40] = b + jnp.where(first_has, 0.25 * north[k, 23:31], 0.0)
+            src[k, 7:8] = edge[0, k : k + 1]
+            src[k, 40:41] = edge[1, k : k + 1]
+            src[k, 16:17] = src[k, 16:17] + 0.25 * edge[0, n_chunks + k : n_chunks + k + 1]
+            src[k, 31:32] = src[k, 31:32] - 0.25 * edge[1, n_chunks + k : n_chunks + k + 1]
 
     def first_sweep():
         weight, inverse = weight_of(8, 2 * ROWS)
@@ -465,12 +469,13 @@
             pltpu.VMEM((n_chunks, 2 * ROWS, LANES), F32),
             pltpu.VMEM((4, ROWS, n_cols), BF16),
             pltpu.VMEM((n_chunks, 3 * ROWS, LANES), F32),
+            pltpu.VMEM((2, 2 * n_chunks, LANES), F32),
             pltpu.VMEM((n_chunks, 2 * ROWS, LANES), F32),
             pltpu.VMEM((2, n_chunks, 3 * ROWS, LANES), F32),
-            pltpu.VMEM((STEPS, n_chunks, ROWS, LANES), BF16),
-            pltpu.VMEM((STEPS, n_chunks, ROWS, LANES), BF16),
-            pltpu.VMEM((STEPS, n_chunks, ROWS, LANES), BF16),
-            pltpu.VMEM((STEPS, n_chunks, ROWS, LANES), BF16),
+            pltpu.VMEM((STEPS, n_chunks + n_chunks // 4, 8, LANES), BF16),
+            pltpu.VMEM((STEPS, n_chunks + n_chunks // 4, 8, LANES), BF16),
+            pltpu.VMEM((STEPS, n_chunks + n_chunks // 4, 8, LANES), BF16),
+            pltpu.VMEM((STEPS, n_chunks + n_chunks // 4, 8, LANES), BF16),
             pltpu.SemaphoreType.DMA((2 + STEPS,)),
             pltpu.SemaphoreType.DMA((4 + STEPS,)),
             pltpu.SemaphoreType.DMA((4 + STEPS,)),

time: 38.4 us -> 37.5 us (0.977)
  Pallas kernels: 37.5 us -> 36.6 us
    pallas_call x1, Pallas kernels: 37.5 us -> 36.6 us  [local(): pl.pallas_call(functools.partial(kernel, n_lon, n_lat), out_shape=jax.Sha...]
where the time goes in v6:
time: 37.5 us; the launch traced here: 37.4 us
  Pallas kernels  36.6 us (98%)
  local copies, waits for them, and re-layouts  0.8 us (2%)
    pallas_call x1, Pallas kernels, local(): pl.pallas_call(functools.partial(kernel, n_lon, n_lat), out_shape=jax.Sha...  36.6 us
    unnamed x1, local copies, waits for them, and re-layouts  0.8 us

profile of v6, /device:TPU:1, one launch (start us, length us, event | category | flops | bytes accessed | tf_op | source)
XLA Modules:
  0.0 37.4 jit_solution(13835187911558328748)
XLA Ops:
  0.0 36.6 %transport.1 = bf16[4,2,128,256]{3,2,1,0:T(8,128)(2,1)S(1)} custom-call(bf16[4,2,128,256]{3,2,1,0:T(8,128)(2,1)} %fields.1, s32[2,8]{1,0:T(2,128)} %shifts_hbm.1, f32[2,128,256]{2,1,0:T(8,128)} %fractions.1, f32[2]{0:T(128)} %helm_hbm.1), custom_call_target="tpu_custom_call" | custom-call | tf_op jit(solution)/shard_map/transport/pallas_call | solution.py:452
  36.6 0.8 %copy.6 = bf16[4,2,128,256]{3,2,1,0:T(8,128)(2,1)} copy(bf16[4,2,128,256]{3,2,1,0:T(8,128)(2,1)S(1)} %transport.1) | data formatting | bytes 1048576

commit v7 on v6

--- a/solution.py
+++ b/solution.py
@@ -77,17 +77,6 @@
     def wrap(w):
         return w & (n_windows - 1)
 
-    barrier = pltpu.get_barrier_semaphore()
-
-    def greet(j, _):
-        peer = lax.rem(lon + j, n_lon)
-        pl.semaphore_signal(barrier, inc=1, device_id={"lon": peer, "lat": lat}, device_id_type=MESH)
-        return 0
-
-    lax.fori_loop(1, n_lon, greet, 0)
-    pl.semaphore_signal(barrier, inc=1, device_id=dev_up, device_id_type=MESH)
-    pl.semaphore_signal(barrier, inc=1, device_id=dev_down, device_id_type=MESH)
-
     get_shifts = pltpu.make_async_copy(shifts_hbm, shifts, small.at[0])
     get_helm = pltpu.make_async_copy(helm_hbm, helm, small.at[1])
     get_fractions = [
@@ -98,23 +87,17 @@
     get_shifts.start()
     get_helm.start()
 
-    row = lax.broadcasted_iota(jnp.int32, (WINDOW, WINDOW), 0)
-    col = lax.broadcasted_iota(jnp.int32, (WINDOW, WINDOW), 1)
-    deal[...] = jnp.where(row == WAYS * ((col & (LANES - 1))) + (col >> 7), 1.0, 0.0).astype(BF16)
-    gather[...] = jnp.where(col == WAYS * ((row & (LANES - 1))) + (row >> 7), 1.0, 0.0).astype(BF16)
-
-    zero = jnp.zeros((8, LANES), F32)
-
-    def clear(base):
-        for j in range(n_chunks):
-            k = base + j
-            north[k, 0:8] = zero
-            north[k, 24:32] = zero
-            for i in range(2):
-                pot[i, k, 0:8] = zero
-                pot[i, k, 40:48] = zero
-
-    clear(0)
+    barrier = pltpu.get_barrier_semaphore()
+
+    def greet(j, _):
+        peer = lax.rem(lon + j, n_lon)
+        pl.semaphore_signal(barrier, inc=1, device_id={"lon": peer, "lat": lat}, device_id_type=MESH)
+        return 0
+
+    lax.fori_loop(1, n_lon, greet, 0, unroll=True)
+    pl.semaphore_signal(barrier, inc=1, device_id=dev_up, device_id_type=MESH)
+    pl.semaphore_signal(barrier, inc=1, device_id=dev_down, device_id_type=MESH)
+
     pl.semaphore_wait(barrier, n_lon + 1)
 
     def in_refs(part, to_block, to_level, from_lon):
@@ -137,7 +120,7 @@
             ).start()
             return 0
 
-        lax.fori_loop(1, n_lon, turn, 0)
+        lax.fori_loop(1, n_lon, turn, 0, unroll=True)
         from_ref, to_ref = in_refs(part, block, level, lon)
         pltpu.make_async_copy(from_ref, to_ref, in_recv.at[part]).start()
 
@@ -164,6 +147,23 @@
     code(1)
     send_part(3)
     send_part(5)
+    row = lax.broadcasted_iota(jnp.int32, (WINDOW, WINDOW), 0)
+    col = lax.broadcasted_iota(jnp.int32, (WINDOW, WINDOW), 1)
+    deal[...] = jnp.where(row == WAYS * ((col & (LANES - 1))) + (col >> 7), 1.0, 0.0).astype(BF16)
+    gather[...] = jnp.where(col == WAYS * ((row & (LANES - 1))) + (row >> 7), 1.0, 0.0).astype(BF16)
+
+    zero = jnp.zeros((8, LANES), F32)
+
+    def clear(base):
+        for j in range(n_chunks):
+            k = base + j
+            north[k, 0:8] = zero
+            north[k, 24:32] = zero
+            for i in range(2):
+                pot[i, k, 0:8] = zero
+                pot[i, k, 40:48] = zero
+
+    clear(0)
     get_shifts.wait()
     get_helm.wait()
 
@@ -369,23 +369,19 @@
         per = WINDOW // tile
         core = lax.rem(lon, 2)
 
-        def turn(j, _):
+        for j in range(1, n_windows + 1):
             w = wrap(lax.div(lon, per) + j + core * (n_windows - 2 * j))
             made = {}
             update(w, 1, lambda f, k, value: made.setdefault(f, []).append(value))
             rows = natural([jnp.concatenate(made[f], axis=1) for f in range(3)])
             for f in range(3):
                 res[f, :, window(w)] = rows[f * ROWS : (f + 1) * ROWS].astype(BF16)
-            for i in range(per):
-                peer = per * w + i
-
-                @pl.when(peer != lon)
-                def _():
-                    out_copy(0, peer).start()
-
-            return 0
-
-        lax.fori_loop(1, n_windows + 1, turn, 0)
+            if j < n_windows:
+                for i in range(per):
+                    out_copy(0, per * w + i).start()
+            else:
+                for i in range(1, per):
+                    out_copy(0, per * w + lax.rem(lon + i, per)).start()
         out_keep(0).start()
 
     def restore(f):
@@ -417,15 +413,15 @@
         advect(step, [3 + step], [functools.partial(to_field, 4 - step)])
         if last:
             restore(3)
-
+        for c in copies:
+            c.wait_recv()
+        if last:
             def send_res3(j, _):
                 out_copy(1, lax.rem(lon + j, n_lon)).start()
                 return 0
 
-            lax.fori_loop(1, n_lon, send_res3, 0)
+            lax.fori_loop(1, n_lon, send_res3, 0, unroll=True)
             out_keep(1).start()
-        for c in copies:
-            c.wait_recv()
         complete(step)
         first_sweep()
         later_sweeps()

time: 37.5 us -> 37 us (0.987)
  Pallas kernels: 36.6 us -> 36.1 us
    pallas_call x1, Pallas kernels: 36.6 us -> 36.1 us  [local(): pl.pallas_call(functools.partial(kernel, n_lon, n_lat), out_shape=jax.Sha...]
where the time goes in v7:
time: 37 us
  Pallas kernels  36.1 us (98%)
  local copies, waits for them, and re-layouts  0.8 us (2%)
    pallas_call x1, Pallas kernels, local(): pl.pallas_call(functools.partial(kernel, n_lon, n_lat), out_shape=jax.Sha...  36.1 us
    unnamed x1, local copies, waits for them, and re-layouts  0.8 us

profile of v7, /device:TPU:1, one launch (start us, length us, event | category | flops | bytes accessed | tf_op | source)
XLA Modules:
  0.0 37.0 jit_solution(14052472902738916326)
XLA Ops:
  0.0 36.1 %transport.1 = bf16[4,2,128,256]{3,2,1,0:T(8,128)(2,1)S(1)} custom-call(bf16[4,2,128,256]{3,2,1,0:T(8,128)(2,1)} %fields.1, s32[2,8]{1,0:T(2,128)} %shifts_hbm.1, f32[2,128,256]{2,1,0:T(8,128)} %fractions.1, f32[2]{0:T(128)} %helm_hbm.1), custom_call_target="tpu_custom_call" | custom-call | tf_op jit(solution)/shard_map/transport/pallas_call | solution.py:448
  36.2 0.8 %copy.6 = bf16[4,2,128,256]{3,2,1,0:T(8,128)(2,1)} copy(bf16[4,2,128,256]{3,2,1,0:T(8,128)(2,1)S(1)} %transport.1) | data formatting | bytes 1048576
